TPU v7x, 512 devices: a whole 4x8x8 slice. The times are simulated.
512 devices in a mesh: state: 8 (over y_lo, x), bond: 64 (over z, y_hi, core).
Axes of the slice: x: 4, y: 8 (y_hi: 4, y_lo: 2; y = y_hi * 2 + y_lo), z: 8, core: 2. Of those that a mesh axis runs over, the one named last changes fastest.
Arguments:
- intersect_left: bfloat16 [8, 2048, 2048], P('state', 'bond'), may hold values from -0.125 to 0.125
- stored_block: bfloat16 [8, 4, 2048, 2048], P('state', None, 'bond'), may hold values from -6 to 6
- stored_site: bfloat16 [8, 2, 2048, 2048], P('state', None, 'bond'), may hold values from -6 to 6
- current_site: bfloat16 [2048, 2, 2048], P('bond', None, 'state'), may hold values from -0.09375 to 0.09375
- current_block: bfloat16 [4, 2048, 2048], P(None, 'bond', 'state'), may hold values from -6 to 6
- penalty_weight: float32 [8], replicated, may hold values from 0.5 to 4
Outputs:
- penalized: float32 [4, 2048, 2048], P(None, 'bond', 'state')
- intersect_next: bfloat16 [8, 2048, 2048], P('state', 'bond')
All inputs are finite; a program needn't handle non-finite values.
Results may differ from a plain program's by a relative error of at most 0.0055.
Values may be sent and summed in bfloat16 or wider, within the bound.
No kernel may reach another device: no remote copies, remote signals or barrier semaphores. Data moves between devices by JAX's collectives and lax.ppermute only.
A program may use at most 64 MiB of HBM per device.

v0:
```python
import jax
import jax.numpy as jnp
from jax import lax
from jax.experimental import pallas as pl
from jax.experimental.pallas import tpu as pltpu
from jax.sharding import Mesh
from jax.sharding import PartitionSpec as P

STATE = ("state_0", "state_1")
ROW = "bond_0"
FAR = "bond_1"
NEAR = "bond_2"
CORE = "bond_3"


ORDER = (0, 1, 7, 6, 2, 5, 3, 4)


def shifted(value, axis, step):
    size = lax.axis_size(axis)
    return lax.ppermute(value, axis, [(i, (i + step) % size) for i in range(size)])


def exchanged(value, axis):
    return lax.all_to_all(value, axis, split_axis=0, concat_axis=0, tiled=True)


def sent_to_all(value, axis):
    return exchanged(jnp.broadcast_to(value, (lax.axis_size(axis), *value.shape)), axis)


def after(value, *others):
    return lax.optimization_barrier((value, *others))[0]


def load_environment(pieces, environment, semaphores):
    rows = environment.shape[0]
    z = lax.axis_index(ROW)
    copies = []

    def load(piece, offset, target=None):
        place = environment.at[lax.rem(z + offset, rows)]
        if target is not None:
            place = place.at[target]
        copies.append(pltpu.make_async_copy(piece, place, semaphores.at[len(copies)]))

    *whole, low, high = pieces
    load(whole[0], 0)
    for step in range(1, rows // 2):
        load(whole[2 * step - 1], rows - step)
        load(whole[2 * step], step)
    split = low.shape[0]
    load(low, rows // 2, pl.ds(0, split))
    load(high, rows // 2, pl.ds(split, split))
    for copy in copies:
        copy.start()
    return copies


def rows_times(left, right):
    return lax.dot_general(left, right, (((1,), (1,)), ((), ())), preferred_element_type=jnp.float32)


def project_kernel(*refs):
    pieces = refs[:9]
    stored = refs[9:13]
    current, out, environment, operand, semaphores = refs[13:]
    v = lax.axis_index(NEAR)
    c = lax.axis_index(CORE)
    copies = []
    for k, (flip_v, flip_c) in enumerate(((0, 0), (1, 0), (0, 1), (1, 1))):
        slot = lax.rem(v + flip_v, 2) * 2 + lax.rem(c + flip_c, 2)
        copies.append(pltpu.make_async_copy(stored[k], operand.at[slot], semaphores.at[9 + k]))
        copies[-1].start()
    copies += load_environment(pieces, environment, semaphores)
    for copy in copies[:4]:
        copy.wait()
    arrived = ((0, 2), (1, 3), (4, 5), (6, 7, 8))
    slots, count, bond = operand.shape
    right = operand[...].reshape(slots * count, bond)
    rows, height, _ = environment.shape
    z = lax.axis_index(ROW)
    total = jnp.zeros((height, count), jnp.float32)
    for step, ready in enumerate(arrived):
        for k in ready:
            copies[4 + k].wait()
        places = [lax.rem(z + offset, rows) for offset in ORDER[2 * step : 2 * step + 2]]
        left = jnp.concatenate([environment[place] for place in places])
        product = rows_times(left, right)
        for i, place in enumerate(places):
            for k in range(slots):
                one = product[i * height : (i + 1) * height, k * count : (k + 1) * count]
                out[place, k, :height] = one.astype(jnp.bfloat16)
                total += one * current[place, k].astype(jnp.float32)
    whole = jnp.full((8, count), jnp.sum(total), jnp.float32)
    high = whole.astype(jnp.bfloat16).astype(jnp.float32)
    middle = (whole - high).astype(jnp.bfloat16).astype(jnp.float32)
    low = whole - high - middle
    row = lax.broadcasted_iota(jnp.int32, whole.shape, 0)
    parts = jnp.where(row == 0, high, jnp.where(row == 1, middle, jnp.where(row == 2, low, 0.0)))
    for i in range(rows):
        for k in range(slots):
            out[i, k, height:] = parts.astype(jnp.bfloat16)


def grow_kernel(*refs):
    pieces = refs[:9]
    mine, other, site, out, environment, operand, moved, semaphores = refs[9:]
    y = lax.axis_index(FAR) * 2 + lax.axis_index(NEAR)
    c = lax.axis_index(CORE)
    copies = load_environment(pieces, environment, semaphores)
    number = len(copies)
    for k, offset in enumerate((0, 3, 1, 2)):
        for flip, source in enumerate((mine, other)):
            slot = lax.rem(y + offset, 4) * 2 + lax.rem(c + flip, 2)
            for s in range(operand.shape[0]):
                copy = pltpu.make_async_copy(
                    source.at[k, s], operand.at[s, slot], semaphores.at[number]
                )
                copy.start()
                copies.append(copy)
                number += 1
    for copy in copies:
        copy.wait()
    physical, slots, count, bond = operand.shape
    block = slots * count
    right = operand[...].reshape(physical * block, bond)
    rows, height, _ = environment.shape
    for z in range(0, rows, 2):
        left = environment[z : z + 2].reshape(2 * height, bond)
        moved[z * height : (z + 2) * height] = rows_times(left, right).astype(jnp.bfloat16)
    for k in range(out.shape[0]):
        total = jnp.zeros(out.shape[1:], jnp.float32)
        for s in range(physical):
            left = site[k, :, s].reshape(rows * height, site.shape[-1])
            total += lax.dot_general(
                left,
                moved[:, s * block : (s + 1) * block],
                (((0,), (0,)), ((), ())),
                preferred_element_type=jnp.float32,
            )
        out[k] = total.astype(jnp.bfloat16)


def whole(intersect_left, stored_block, stored_site, current_site, current_block, penalty_weight):
    states = lax.axis_size(STATE)
    rows = lax.axis_size(ROW)
    pairs, width, bond = stored_block.shape[1:]
    physical = stored_site.shape[1]
    block = current_block.shape[2]
    slots = 4
    count = pairs * width
    height = 2 * width
    half = block // 2
    group = (*STATE, NEAR, CORE)
    anywhere = pl.BlockSpec(memory_space=pl.ANY)
    resident = pl.BlockSpec(memory_space=pltpu.VMEM)

    turned = current_block.reshape(count, block).T.reshape(2, slots, width, count)
    turned = turned.transpose(1, 0, 2, 3).reshape(slots, height, count)
    turned = jnp.broadcast_to(turned, (states, *turned.shape)).reshape(-1, height, count)
    current = exchanged(turned, group).reshape(states, slots, height, count)

    site = current_site.reshape(width, physical, 2, half).transpose(2, 1, 0, 3)
    first = lax.axis_index(FAR) == 0
    kept = jnp.where(first, site[0], site[1])
    got = shifted(jnp.where(first, site[1], site[0]), FAR, 1)
    site = jnp.where(first, jnp.stack([kept, got]), jnp.stack([got, kept]))
    site = site.transpose(1, 0, 2, 3).reshape(physical, height, half)
    site = sent_to_all(site, ROW)
    site = sent_to_all(site, STATE)

    mine = intersect_left[0]
    other = shifted(mine, FAR, 1)
    environment = jnp.where(first, jnp.stack([mine, other]), jnp.stack([other, mine]))
    environment = environment.reshape(height, bond)
    pieces = [environment]
    below = above = environment
    for _ in range(1, rows // 2):
        below = shifted(below, ROW, 1)
        above = shifted(above, ROW, -1)
        pieces += [below, above]
    low = shifted(below[:width], ROW, 1)
    high = shifted(above[width:], ROW, -1)
    pieces += [low, high]

    stored = stored_block[0].reshape(count, bond)
    stored_core = shifted(stored, CORE, 1)
    stored_near = shifted(after(stored, other), NEAR, 1)
    stored_both = shifted(stored_near, CORE, 1)

    column = (FAR, NEAR)
    local = after(stored_site[0].reshape(physical * width, bond), stored_near)
    left = shifted(local, column, 1)
    right = shifted(local, column, -1)
    left_rows, right_rows = left[:width], right[width:]
    left_far = shifted(left_rows, column, 1)
    right_far = shifted(right_rows, column, -1)
    local = jnp.concatenate([local, left, right, left_far, right_far])
    across = shifted(local, CORE, 1)
    local = local.reshape(4, physical, width, bond)
    across = across.reshape(4, physical, width, bond)

    projected = pl.pallas_call(
        project_kernel,
        out_shape=jax.ShapeDtypeStruct((rows, slots, height + 8, count), jnp.bfloat16),
        in_specs=[anywhere] * 13 + [resident],
        out_specs=resident,
        scratch_shapes=[
            pltpu.VMEM((rows, height, bond), jnp.bfloat16),
            pltpu.VMEM((slots, count, bond), jnp.bfloat16),
            pltpu.SemaphoreType.DMA((13,)),
        ],
        cost_estimate=pl.CostEstimate(flops=2 * 512 * 512 * 2048, bytes_accessed=5 << 20, transcendentals=0),
        name="project",
    )(*pieces, stored, stored_near, stored_core, stored_both, current)

    received = exchanged(projected.reshape(-1, height + 8, count), group)
    received = received.reshape(states, slots, height + 8, count).astype(jnp.float32)
    total = received[:, :, height : height + 3].sum(axis=(1, 2))
    total = sent_to_all(total, (ROW, FAR))
    intersect = total.sum(axis=0)[:, 0] * (1.0 / (physical * bond))

    grown = pl.pallas_call(
        grow_kernel,
        out_shape=jax.ShapeDtypeStruct((states, half, block), jnp.bfloat16),
        in_specs=[anywhere] * 11 + [resident],
        out_specs=resident,
        scratch_shapes=[
            pltpu.VMEM((rows, height, bond), jnp.bfloat16),
            pltpu.VMEM((physical, 8, width, bond), jnp.bfloat16),
            pltpu.VMEM((rows * height, physical * block), jnp.bfloat16),
            pltpu.SemaphoreType.DMA((25,)),
        ],
        cost_estimate=pl.CostEstimate(flops=3 * 512 * 512 * 2048, bytes_accessed=6 << 20, transcendentals=0),
        name="grow",
    )(*pieces, local, across, site)

    grown = exchanged(grown.reshape(states * slots, width, block), (ROW, NEAR, CORE))
    grown = grown.reshape(rows, slots, width, block).astype(jnp.float32).sum(axis=1)
    intersect_next = grown.astype(jnp.bfloat16).transpose(1, 0, 2).reshape(1, width, rows * block)

    gain = penalty_weight * intersect
    summed = jnp.sum(gain[:, None, None, None] * received[:, :, :height], axis=0)
    summed = summed.reshape(slots, 2, width, count).transpose(1, 0, 2, 3).reshape(block, count)
    penalized = current_block.astype(jnp.float32) + summed.T.reshape(pairs, width, block)
    return (penalized, intersect_next)


def solution(mesh):
    torus = Mesh(
        mesh.devices.reshape(2, mesh.shape["state"] // 2, 8, 2, 2, 2),
        (*STATE, ROW, FAR, NEAR, CORE),
    )
    bond = (ROW, FAR, NEAR, CORE)
    in_specs = (
        P(STATE, bond, None),
        P(STATE, None, bond, None),
        P(STATE, None, bond, None),
        P(bond, None, STATE),
        P(None, bond, STATE),
        P(),
    )
    out_specs = (P(None, bond, STATE), P(STATE, bond, None))
    return jax.shard_map(whole, mesh=torus, in_specs=in_specs, out_specs=out_specs, check_vma=False)
```

profile of v0, /device:TPU:63, one launch (start us, length us, event | category | flops | bytes accessed | tf_op | source)
XLA Modules:
  0.0 236.9 jit_solution(8766493500036977742)
XLA Ops:
  2.6 8.0 %all-to-all-start = ((bf16[32,64,128]{2,1,0:T(8,128)(2,1)}), bf16[32,64,128]{2,1,0:T(8,128)(2,1)S(1)}, u32[]{:S(2)}, u32[]{:S(2)}) async-start(bf16[32,64,128]{2,1,0:T(8,128)(2,1)} %bitcast.9), calls=%async_computation | async-start | bytes 1048576 | tf_op jit(solution)/shard_map/all_to_all | solution.py:25
  10.6 5.9 %collective-permute-start = (bf16[32,2048]{1,0:T(8,128)(2,1)S(1)}, bf16[32,2048]{1,0:T(8,128)(2,1)S(1)}, u32[]{:S(2)}, u32[]{:S(2)}) collective-permute-start(bf16[32,2048]{1,0:T(8,128)(2,1)S(1)} %bitcast.62), channel_id=1, source_target_pairs={{0,4},{4,0},{1,5},{5,1},{2,6},{6,2},{3,7},{7,3},{8,12},{12,8},{9,1... | collective-permute-start | bytes 393224 | tf_op jit(solution)/shard_map/ppermute | solution.py:21
  16.6 12.9 %collective-permute-done = bf16[32,2048]{1,0:T(8,128)(2,1)S(1)} collective-permute-done((bf16[32,2048]{1,0:T(8,128)(2,1)S(1)}, bf16[32,2048]{1,0:T(8,128)(2,1)S(1)}, u32[]{:S(2)}, u32[]{:S(2)}) %collective-permute-start) | collective-permute-done | bytes 131104 | tf_op jit(solution)/shard_map/ppermute | solution.py:21
  31.5 9.2 %collective-permute-start.2 = (bf16[64,2048]{1,0:T(8,128)(2,1)S(1)}, bf16[64,2048]{1,0:T(8,128)(2,1)S(1)}, u32[]{:S(2)}, u32[]{:S(2)}) collective-permute-start(bf16[64,2048]{1,0:T(8,128)(2,1)S(1)} %bitcast.42), channel_id=1, source_target_pairs={{0,56},{8,0},{16,8},{24,16},{32,24},{40,32},{48,40},{56,48},{1,57}... | collective-permute-start | bytes 786440 | tf_op jit(solution)/shard_map/ppermute | solution.py:21
  45.3 5.3 %collective-permute-start.4 = (bf16[64,2048]{1,0:T(8,128)(2,1)S(1)}, bf16[64,2048]{1,0:T(8,128)(2,1)S(1)}, u32[]{:S(2)}, u32[]{:S(2)}) collective-permute-start(bf16[64,2048]{1,0:T(8,128)(2,1)S(1)} %collective-permute-done.2.refs_2_), channel_id=1, source_target_pairs={{0,56},{8,0},{16,8},{24,16},{32,24},{40,32},{48,40},{56,48},{1,57}... | collective-permute-start | bytes 786440 | tf_op jit(solution)/shard_map/ppermute | solution.py:21
  52.6 4.0 %collective-permute-start.10 = (bf16[128,2048]{1,0:T(8,128)(2,1)S(1)}, bf16[128,2048]{1,0:T(8,128)(2,1)}, u32[]{:S(2)}, u32[]{:S(2)}) collective-permute-start(bf16[128,2048]{1,0:T(8,128)(2,1)S(1)} %bitcast.54), channel_id=1, source_target_pairs={{0,1},{1,0},{2,3},{3,2},{4,5},{5,4},{6,7},{7,6},{8,9},{9,8},{10,11... | collective-permute-start | bytes 1572872 | tf_op jit(solution)/shard_map/ppermute | solution.py:21
  58.7 4.8 %collective-permute-start.17 = (bf16[2,32,128]{2,1,0:T(8,128)(2,1)S(1)}, bf16[2,32,128]{2,1,0:T(8,128)(2,1)S(1)}, u32[]{:S(2)}, u32[]{:S(2)}) collective-permute-start(bf16[2,32,128]{2,1,0:T(8,128)(2,1)S(1)} %bitcast.65), channel_id=1, source_target_pairs={{0,4},{4,0},{1,5},{5,1},{2,6},{6,2},{3,7},{7,3},{8,12},{12,8},{9,1... | collective-permute-start | bytes 49160 | tf_op jit(solution)/shard_map/ppermute | solution.py:21
  63.5 3.6 %collective-permute-done.17 = bf16[2,32,128]{2,1,0:T(8,128)(2,1)S(1)} collective-permute-done((bf16[2,32,128]{2,1,0:T(8,128)(2,1)S(1)}, bf16[2,32,128]{2,1,0:T(8,128)(2,1)S(1)}, u32[]{:S(2)}, u32[]{:S(2)}) %collective-permute-start.17) | collective-permute-done | bytes 16416 | tf_op jit(solution)/shard_map/ppermute | solution.py:21
  67.1 8.2 %collective-permute-start.6 = (bf16[64,2048]{1,0:T(8,128)(2,1)S(1)}, bf16[64,2048]{1,0:T(8,128)(2,1)S(1)}, u32[]{:S(2)}, u32[]{:S(2)}) collective-permute-start(bf16[64,2048]{1,0:T(8,128)(2,1)S(1)} %collective-permute-done.4.refs_4_), channel_id=1, source_target_pairs={{0,56},{8,0},{16,8},{24,16},{32,24},{40,32},{48,40},{56,48},{1,57}... | collective-permute-start | bytes 786440 | tf_op jit(solution)/shard_map/ppermute | solution.py:21
  78.4 3.9 %all-to-all-start.3 = ((bf16[8,2,64,128]{3,2,1,0:T(8,128)(2,1)}), bf16[8,2,64,128]{3,2,1,0:T(8,128)(2,1)S(1)}, u32[]{:S(2)}, u32[]{:S(2)}) async-start(bf16[8,2,64,128]{3,2,1,0:T(8,128)(2,1)} %broadcast_in_dim.15), calls=%async_computation.3 | async-start | bytes 524288 | tf_op jit(solution)/shard_map/all_to_all | solution.py:25
  82.4 4.6 %collective-permute-start.8 = (bf16[32,2048]{1,0:T(8,128)(2,1)S(1)}, bf16[32,2048]{1,0:T(8,128)(2,1)S(1)}, u32[]{:S(2)}, u32[]{:S(2)}) collective-permute-start(bf16[32,2048]{1,0:T(8,128)(2,1)S(1)} %slice.39), channel_id=1, source_target_pairs={{0,56},{8,0},{16,8},{24,16},{32,24},{40,32},{48,40},{56,48},{1,57}... | collective-permute-start | bytes 393224 | tf_op jit(solution)/shard_map/ppermute | solution.py:21
  91.1 3.3 %collective-permute-done.7.refs_7_ = bf16[32,2048]{1,0:T(8,128)(2,1)S(1)} collective-permute-done((bf16[32,2048]{1,0:T(8,128)(2,1)S(1)}, bf16[32,2048]{1,0:T(8,128)(2,1)S(1)}, u32[]{:S(2)}, u32[]{:S(2)}) %collective-permute-start.7) | collective-permute-done | bytes 131104 | tf_op jit(solution)/shard_map/ppermute | solution.py:21
  95.1 7.1 %project.1 = bf16[8,4,72,128]{3,2,1,0:T(8,128)(2,1)} custom-call(bf16[64,2048]{1,0:T(8,128)(2,1)} %bitcast.44, bf16[64,2048]{1,0:T(8,128)(2,1)} %copy-done.7, bf16[64,2048]{1,0:T(8,128)(2,1)} %copy-done.6, bf16[64,2048]{1,0:T(8,128)(2,1)} %copy-done.9, bf16[64,2048]{1,0:T(8,128)(2,1)} %copy-done.8, bf16[64,2048]{1,0:T(8,128)(2,1)} %copy-done.5, ...), custom_call_target="tpu_custom_call" | custom-call | flops 1073741824 | bytes 5242880 | tf_op jit(solution)/shard_map/project/pallas_call | solution.py:204
  102.1 24.7 %all_to_all.30 = bf16[32,72,128]{2,1,0:T(8,128)(2,1)} all-to-all(bf16[32,72,128]{2,1,0:T(8,128)(2,1)} %bitcast.41), channel_id=1, replica_groups=mesh['state_0'=2,'state_1'=4,'bond_0'=8,'bond_1'=2,'bond_2'=2,'bond_3'=2..., dimensions={0} | all-to-all | bytes 1179648 | tf_op jit(solution)/shard_map/all_to_all | solution.py:25
  128.7 5.3 %all-to-all-start.4 = ((bf16[8,8,2,64,128]{4,3,2,1,0:T(8,128)(2,1)}), bf16[8,8,2,64,128]{4,3,2,1,0:T(8,128)(2,1)S(1)}, u32[]{:S(2)}, u32[]{:S(2)}) async-start(bf16[8,8,2,64,128]{4,3,2,1,0:T(8,128)(2,1)} %broadcast_in_dim.16), calls=%async_computation.4 | async-start | bytes 4194304 | tf_op jit(solution)/shard_map/all_to_all | solution.py:25
  134.0 4.0 %collective-permute-start.13 = (bf16[64,2048]{1,0:T(8,128)(2,1)S(1)}, bf16[64,2048]{1,0:T(8,128)(2,1)S(1)}, u32[]{:S(2)}, u32[]{:S(2)}) collective-permute-start(bf16[64,2048]{1,0:T(8,128)(2,1)S(1)} %bitcast.58), channel_id=1, source_target_pairs={{0,6},{2,0},{4,2},{6,4},{1,7},{3,1},{5,3},{7,5},{8,14},{10,8},{12,... | collective-permute-start | bytes 786440 | tf_op jit(solution)/shard_map/ppermute | solution.py:21
  138.0 3.3 %collective-permute-start.12 = (bf16[64,2048]{1,0:T(8,128)(2,1)S(1)}, bf16[64,2048]{1,0:T(8,128)(2,1)S(1)}, u32[]{:S(2)}, u32[]{:S(2)}) collective-permute-start(bf16[64,2048]{1,0:T(8,128)(2,1)S(1)} %bitcast.59), channel_id=1, source_target_pairs={{0,2},{2,4},{4,6},{6,0},{1,3},{3,5},{5,7},{7,1},{8,10},{10,12},{12... | collective-permute-start | bytes 786440 | tf_op jit(solution)/shard_map/ppermute | solution.py:21
  142.1 31.5 %collective-permute-done.13 = bf16[64,2048]{1,0:T(8,128)(2,1)S(1)} collective-permute-done((bf16[64,2048]{1,0:T(8,128)(2,1)S(1)}, bf16[64,2048]{1,0:T(8,128)(2,1)S(1)}, u32[]{:S(2)}, u32[]{:S(2)}) %collective-permute-start.13) | collective-permute-done | bytes 262176 | tf_op jit(solution)/shard_map/ppermute | solution.py:21
  175.5 5.5 %collective-permute-start.14 = (bf16[32,2048]{1,0:T(8,128)(2,1)S(1)}, bf16[32,2048]{1,0:T(8,128)(2,1)S(1)}, u32[]{:S(2)}, u32[]{:S(2)}) collective-permute-start(bf16[32,2048]{1,0:T(8,128)(2,1)S(1)} %slice.42), channel_id=1, source_target_pairs={{0,2},{2,4},{4,6},{6,0},{1,3},{3,5},{5,7},{7,1},{8,10},{10,12},{12... | collective-permute-start | bytes 393224 | tf_op jit(solution)/shard_map/ppermute | solution.py:21
  184.3 4.9 %collective-permute-start.16 = (bf16[256,2048]{1,0:T(8,128)(2,1)}, bf16[256,2048]{1,0:T(8,128)(2,1)}, u32[]{:S(2)}, u32[]{:S(2)}) collective-permute-start(bf16[256,2048]{1,0:T(8,128)(2,1)} %constant_dynamic-update-slice_fusion), channel_id=1, source_target_pairs={{0,1},{1,0},{2,3},{3,2},{4,5},{5,4},{6,7},{7,6},{8,9},{9,8},{10,11... | collective-permute-start | bytes 3145736 | tf_op jit(solution)/shard_map/ppermute | solution.py:21
  190.1 9.4 %all-to-all-start.2 = ((f32[16,8,128]{2,1,0:T(8,128)}), f32[16,8,128]{2,1,0:T(8,128)S(1)}, u32[]{:S(2)}, u32[]{:S(2)}) async-start(f32[16,8,128]{2,1,0:T(8,128)} %broadcast_in_dim.14), calls=%async_computation.2 | async-start | bytes 131072 | tf_op jit(solution)/shard_map/all_to_all | solution.py:25
  199.5 8.3 %grow.1 = bf16[8,128,256]{2,1,0:T(8,128)(2,1)} custom-call(bf16[64,2048]{1,0:T(8,128)(2,1)} %bitcast.45, bf16[64,2048]{1,0:T(8,128)(2,1)} %copy-done.7, bf16[64,2048]{1,0:T(8,128)(2,1)} %copy-done.6, bf16[64,2048]{1,0:T(8,128)(2,1)} %copy-done.9, bf16[64,2048]{1,0:T(8,128)(2,1)} %copy-done.8, bf16[64,2048]{1,0:T(8,128)(2,1)} %copy-done.5, ...), custom_call_target="tpu_custom_call" | custom-call | flops 1610612736 | bytes 6291456 | tf_op jit(solution)/shard_map/grow/pallas_call | solution.py:224
  207.8 11.0 %all-to-all-start.5 = ((bf16[32,32,256]{2,1,0:T(8,128)(2,1)}), bf16[32,32,256]{2,1,0:T(8,128)(2,1)S(1)}, u32[]{:S(2)}, u32[]{:S(2)}) async-start(bf16[32,32,256]{2,1,0:T(8,128)(2,1)} %bitcast.47), calls=%async_computation.5 | async-start | bytes 1048576 | tf_op jit(solution)/shard_map/all_to_all | solution.py:25
  219.9 16.1 %all-to-all-done.5 = bf16[32,32,256]{2,1,0:T(8,128)(2,1)S(1)} async-done(((bf16[32,32,256]{2,1,0:T(8,128)(2,1)}), bf16[32,32,256]{2,1,0:T(8,128)(2,1)S(1)}, u32[]{:S(2)}, u32[]{:S(2)}) %all-to-all-start.5) | async-done | bytes 524320 | tf_op jit(solution)/shard_map/all_to_all | solution.py:25
  (96 shorter events, 30.8 us)
Async XLA Ops:
  2.6 74.9 %all-to-all-start = ((bf16[32,64,128]{2,1,0:T(8,128)(2,1)}), bf16[32,64,128]{2,1,0:T(8,128)(2,1)S(1)}, u32[]{:S(2)}, u32[]{:S(2)}) async-start(bf16[32,64,128]{2,1,0:T(8,128)(2,1)} %bitcast.9), calls=%async_computation | async-start | bytes 1048576 | tf_op jit(solution)/shard_map/all_to_all | solution.py:25
  10.6 18.8 %collective-permute-start = (bf16[32,2048]{1,0:T(8,128)(2,1)S(1)}, bf16[32,2048]{1,0:T(8,128)(2,1)S(1)}, u32[]{:S(2)}, u32[]{:S(2)}) collective-permute-start(bf16[32,2048]{1,0:T(8,128)(2,1)S(1)} %bitcast.62), channel_id=1, source_target_pairs={{0,4},{4,0},{1,5},{5,1},{2,6},{6,2},{3,7},{7,3},{8,12},{12,8},{9,1... | collective-permute-start | bytes 393224 | tf_op jit(solution)/shard_map/ppermute | solution.py:21
  29.5 27.2 %collective-permute-start.9 = (bf16[128,2048]{1,0:T(8,128)(2,1)S(1)}, bf16[128,2048]{1,0:T(8,128)(2,1)}, u32[]{:S(2)}, u32[]{:S(2)}) collective-permute-start(bf16[128,2048]{1,0:T(8,128)(2,1)S(1)} %bitcast.53), channel_id=1, source_target_pairs={{0,2},{2,0},{1,3},{3,1},{4,6},{6,4},{5,7},{7,5},{8,10},{10,8},{9,1... | collective-permute-start | bytes 1572872 | tf_op jit(solution)/shard_map/ppermute | solution.py:21
  31.4 63.0 %copy-start.2 = (bf16[2,32,2048]{2,1,0:T(8,128)(2,1)}, bf16[2,32,2048]{2,1,0:T(8,128)(2,1)S(1)}, u32[]{:S(2)}) copy-start(bf16[2,32,2048]{2,1,0:T(8,128)(2,1)S(1)} %maximum_select_fusion) | copy-start | bytes 786436
  31.5 13.8 %collective-permute-start.2 = (bf16[64,2048]{1,0:T(8,128)(2,1)S(1)}, bf16[64,2048]{1,0:T(8,128)(2,1)S(1)}, u32[]{:S(2)}, u32[]{:S(2)}) collective-permute-start(bf16[64,2048]{1,0:T(8,128)(2,1)S(1)} %bitcast.42), channel_id=1, source_target_pairs={{0,56},{8,0},{16,8},{24,16},{32,24},{40,32},{48,40},{56,48},{1,57}... | collective-permute-start | bytes 786440 | tf_op jit(solution)/shard_map/ppermute | solution.py:21
  40.6 10.0 %collective-permute-start.1 = (bf16[64,2048]{1,0:T(8,128)(2,1)S(1)}, bf16[64,2048]{1,0:T(8,128)(2,1)S(1)}, u32[]{:S(2)}, u32[]{:S(2)}) collective-permute-start(bf16[64,2048]{1,0:T(8,128)(2,1)S(1)} %bitcast.43), channel_id=1, source_target_pairs={{0,8},{8,16},{16,24},{24,32},{32,40},{40,48},{48,56},{56,0},{1,9},... | collective-permute-start | bytes 786440 | tf_op jit(solution)/shard_map/ppermute | solution.py:21
  45.3 21.8 %collective-permute-start.4 = (bf16[64,2048]{1,0:T(8,128)(2,1)S(1)}, bf16[64,2048]{1,0:T(8,128)(2,1)S(1)}, u32[]{:S(2)}, u32[]{:S(2)}) collective-permute-start(bf16[64,2048]{1,0:T(8,128)(2,1)S(1)} %collective-permute-done.2.refs_2_), channel_id=1, source_target_pairs={{0,56},{8,0},{16,8},{24,16},{32,24},{40,32},{48,40},{56,48},{1,57}... | collective-permute-start | bytes 786440 | tf_op jit(solution)/shard_map/ppermute | solution.py:21
  50.6 24.8 %collective-permute-start.3 = (bf16[64,2048]{1,0:T(8,128)(2,1)S(1)}, bf16[64,2048]{1,0:T(8,128)(2,1)S(1)}, u32[]{:S(2)}, u32[]{:S(2)}) collective-permute-start(bf16[64,2048]{1,0:T(8,128)(2,1)S(1)} %collective-permute-done.1.refs_1_), channel_id=1, source_target_pairs={{0,8},{8,16},{16,24},{24,32},{32,40},{40,48},{48,56},{56,0},{1,9},... | collective-permute-start | bytes 786440 | tf_op jit(solution)/shard_map/ppermute | solution.py:21
  52.6 36.4 %collective-permute-start.10 = (bf16[128,2048]{1,0:T(8,128)(2,1)S(1)}, bf16[128,2048]{1,0:T(8,128)(2,1)}, u32[]{:S(2)}, u32[]{:S(2)}) collective-permute-start(bf16[128,2048]{1,0:T(8,128)(2,1)S(1)} %bitcast.54), channel_id=1, source_target_pairs={{0,1},{1,0},{2,3},{3,2},{4,5},{5,4},{6,7},{7,6},{8,9},{9,8},{10,11... | collective-permute-start | bytes 1572872 | tf_op jit(solution)/shard_map/ppermute | solution.py:21
  56.7 37.7 %collective-permute-start.11 = (bf16[128,2048]{1,0:T(8,128)(2,1)}, bf16[128,2048]{1,0:T(8,128)(2,1)}, u32[]{:S(2)}, u32[]{:S(2)}) collective-permute-start(bf16[128,2048]{1,0:T(8,128)(2,1)} %collective-permute-done.9.refs_10_), channel_id=1, source_target_pairs={{0,1},{1,0},{2,3},{3,2},{4,5},{5,4},{6,7},{7,6},{8,9},{9,8},{10,11... | collective-permute-start | bytes 1572872 | tf_op jit(solution)/shard_map/ppermute | solution.py:21
  58.7 8.4 %collective-permute-start.17 = (bf16[2,32,128]{2,1,0:T(8,128)(2,1)S(1)}, bf16[2,32,128]{2,1,0:T(8,128)(2,1)S(1)}, u32[]{:S(2)}, u32[]{:S(2)}) collective-permute-start(bf16[2,32,128]{2,1,0:T(8,128)(2,1)S(1)} %bitcast.65), channel_id=1, source_target_pairs={{0,4},{4,0},{1,5},{5,1},{2,6},{6,2},{3,7},{7,3},{8,12},{12,8},{9,1... | collective-permute-start | bytes 49160 | tf_op jit(solution)/shard_map/ppermute | solution.py:21
  67.1 15.2 %collective-permute-start.6 = (bf16[64,2048]{1,0:T(8,128)(2,1)S(1)}, bf16[64,2048]{1,0:T(8,128)(2,1)S(1)}, u32[]{:S(2)}, u32[]{:S(2)}) collective-permute-start(bf16[64,2048]{1,0:T(8,128)(2,1)S(1)} %collective-permute-done.4.refs_4_), channel_id=1, source_target_pairs={{0,56},{8,0},{16,8},{24,16},{32,24},{40,32},{48,40},{56,48},{1,57}... | collective-permute-start | bytes 786440 | tf_op jit(solution)/shard_map/ppermute | solution.py:21
  75.4 11.5 %collective-permute-start.5 = (bf16[64,2048]{1,0:T(8,128)(2,1)S(1)}, bf16[64,2048]{1,0:T(8,128)(2,1)S(1)}, u32[]{:S(2)}, u32[]{:S(2)}) collective-permute-start(bf16[64,2048]{1,0:T(8,128)(2,1)S(1)} %collective-permute-done.3.refs_3_), channel_id=1, source_target_pairs={{0,8},{8,16},{16,24},{24,32},{32,40},{40,48},{48,56},{56,0},{1,9},... | collective-permute-start | bytes 786440 | tf_op jit(solution)/shard_map/ppermute | solution.py:21
  78.4 23.7 %all-to-all-start.3 = ((bf16[8,2,64,128]{3,2,1,0:T(8,128)(2,1)}), bf16[8,2,64,128]{3,2,1,0:T(8,128)(2,1)S(1)}, u32[]{:S(2)}, u32[]{:S(2)}) async-start(bf16[8,2,64,128]{3,2,1,0:T(8,128)(2,1)} %broadcast_in_dim.15), calls=%async_computation.3 | async-start | bytes 524288 | tf_op jit(solution)/shard_map/all_to_all | solution.py:25
  82.4 8.7 %collective-permute-start.8 = (bf16[32,2048]{1,0:T(8,128)(2,1)S(1)}, bf16[32,2048]{1,0:T(8,128)(2,1)S(1)}, u32[]{:S(2)}, u32[]{:S(2)}) collective-permute-start(bf16[32,2048]{1,0:T(8,128)(2,1)S(1)} %slice.39), channel_id=1, source_target_pairs={{0,56},{8,0},{16,8},{24,16},{32,24},{40,32},{48,40},{56,48},{1,57}... | collective-permute-start | bytes 393224 | tf_op jit(solution)/shard_map/ppermute | solution.py:21
  87.0 7.4 %collective-permute-start.7 = (bf16[32,2048]{1,0:T(8,128)(2,1)S(1)}, bf16[32,2048]{1,0:T(8,128)(2,1)S(1)}, u32[]{:S(2)}, u32[]{:S(2)}) collective-permute-start(bf16[32,2048]{1,0:T(8,128)(2,1)S(1)} %slice.38), channel_id=1, source_target_pairs={{0,8},{8,16},{16,24},{24,32},{32,40},{40,48},{48,56},{56,0},{1,9},... | collective-permute-start | bytes 393224 | tf_op jit(solution)/shard_map/ppermute | solution.py:21
  128.7 60.7 %all-to-all-start.4 = ((bf16[8,8,2,64,128]{4,3,2,1,0:T(8,128)(2,1)}), bf16[8,8,2,64,128]{4,3,2,1,0:T(8,128)(2,1)S(1)}, u32[]{:S(2)}, u32[]{:S(2)}) async-start(bf16[8,8,2,64,128]{4,3,2,1,0:T(8,128)(2,1)} %broadcast_in_dim.16), calls=%async_computation.4 | async-start | bytes 4194304 | tf_op jit(solution)/shard_map/all_to_all | solution.py:25
  134.0 39.6 %collective-permute-start.13 = (bf16[64,2048]{1,0:T(8,128)(2,1)S(1)}, bf16[64,2048]{1,0:T(8,128)(2,1)S(1)}, u32[]{:S(2)}, u32[]{:S(2)}) collective-permute-start(bf16[64,2048]{1,0:T(8,128)(2,1)S(1)} %bitcast.58), channel_id=1, source_target_pairs={{0,6},{2,0},{4,2},{6,4},{1,7},{3,1},{5,3},{7,5},{8,14},{10,8},{12,... | collective-permute-start | bytes 786440 | tf_op jit(solution)/shard_map/ppermute | solution.py:21
  138.0 37.5 %collective-permute-start.12 = (bf16[64,2048]{1,0:T(8,128)(2,1)S(1)}, bf16[64,2048]{1,0:T(8,128)(2,1)S(1)}, u32[]{:S(2)}, u32[]{:S(2)}) collective-permute-start(bf16[64,2048]{1,0:T(8,128)(2,1)S(1)} %bitcast.59), channel_id=1, source_target_pairs={{0,2},{2,4},{4,6},{6,0},{1,3},{3,5},{5,7},{7,1},{8,10},{10,12},{12... | collective-permute-start | bytes 786440 | tf_op jit(solution)/shard_map/ppermute | solution.py:21
  173.6 10.1 %collective-permute-start.15 = (bf16[32,2048]{1,0:T(8,128)(2,1)S(1)}, bf16[32,2048]{1,0:T(8,128)(2,1)S(1)}, u32[]{:S(2)}, u32[]{:S(2)}) collective-permute-start(bf16[32,2048]{1,0:T(8,128)(2,1)S(1)} %slice.43), channel_id=1, source_target_pairs={{0,6},{2,0},{4,2},{6,4},{1,7},{3,1},{5,3},{7,5},{8,14},{10,8},{12,... | collective-permute-start | bytes 393224 | tf_op jit(solution)/shard_map/ppermute | solution.py:21
  175.5 7.4 %collective-permute-start.14 = (bf16[32,2048]{1,0:T(8,128)(2,1)S(1)}, bf16[32,2048]{1,0:T(8,128)(2,1)S(1)}, u32[]{:S(2)}, u32[]{:S(2)}) collective-permute-start(bf16[32,2048]{1,0:T(8,128)(2,1)S(1)} %slice.42), channel_id=1, source_target_pairs={{0,2},{2,4},{4,6},{6,0},{1,3},{3,5},{5,7},{7,1},{8,10},{10,12},{12... | collective-permute-start | bytes 393224 | tf_op jit(solution)/shard_map/ppermute | solution.py:21
  184.3 15.1 %collective-permute-start.16 = (bf16[256,2048]{1,0:T(8,128)(2,1)}, bf16[256,2048]{1,0:T(8,128)(2,1)}, u32[]{:S(2)}, u32[]{:S(2)}) collective-permute-start(bf16[256,2048]{1,0:T(8,128)(2,1)} %constant_dynamic-update-slice_fusion), channel_id=1, source_target_pairs={{0,1},{1,0},{2,3},{3,2},{4,5},{5,4},{6,7},{7,6},{8,9},{9,8},{10,11... | collective-permute-start | bytes 3145736 | tf_op jit(solution)/shard_map/ppermute | solution.py:21
  190.1 17.7 %all-to-all-start.2 = ((f32[16,8,128]{2,1,0:T(8,128)}), f32[16,8,128]{2,1,0:T(8,128)S(1)}, u32[]{:S(2)}, u32[]{:S(2)}) async-start(f32[16,8,128]{2,1,0:T(8,128)} %broadcast_in_dim.14), calls=%async_computation.2 | async-start | bytes 131072 | tf_op jit(solution)/shard_map/all_to_all | solution.py:25
  207.8 28.2 %all-to-all-start.5 = ((bf16[32,32,256]{2,1,0:T(8,128)(2,1)}), bf16[32,32,256]{2,1,0:T(8,128)(2,1)S(1)}, u32[]{:S(2)}, u32[]{:S(2)}) async-start(bf16[32,32,256]{2,1,0:T(8,128)(2,1)} %bitcast.47), calls=%async_computation.5 | async-start | bytes 1048576 | tf_op jit(solution)/shard_map/all_to_all | solution.py:25
  (17 other events, 367.0 us)
where the time goes:
time: 238 us; the launch traced here: 237 us
  starting transfers between devices  111 us (47%)
  waiting for transfers between devices  72.9 us (31%)
  blocking collectives  24.7 us (10%)
  Pallas kernels  15.4 us (6%)
  local copies, waits for them, and re-layouts  10.5 us (4%)
    ppermute x18, starting transfers between devices, shifted(): lax.ppermute(value, axis, [(i, (i + step) % size) for i in range(size)])  73.2 us
    ppermute x18, waiting for transfers between devices, shifted(): lax.ppermute(value, axis, [(i, (i + step) % size) for i in range(size)])  56.8 us
    all_to_all x5, starting transfers between devices, exchanged(): return lax.all_to_all(value, axis, split_axis=0, concat_axis=0, tiled=True)  37.6 us
    all_to_all x1, blocking collectives, exchanged(): return lax.all_to_all(value, axis, split_axis=0, concat_axis=0, tiled=True)  24.7 us
    all_to_all x5, waiting for transfers between devices, exchanged(): return lax.all_to_all(value, axis, split_axis=0, concat_axis=0, tiled=True)  16.1 us
    pallas_call x1, Pallas kernels, whole(): pl.pallas_call(grow_kernel, out_shape=jax.ShapeDtypeStruct((states, half,...  8.3 us
    pallas_call x1, Pallas kernels, whole(): pl.pallas_call(project_kernel, out_shape=jax.ShapeDtypeStruct((rows, slot...  7.06 us
  transfers between devices with their start and end apart: 23, of which 8 were waited for; matrix products, arithmetic and copies ran while one was open for 3% of the time, Pallas kernels for 6%

commit v1 on v0

v1 whole, which is shorter than its diff:
```python
import jax
import jax.numpy as jnp
from jax import lax
from jax.experimental import pallas as pl
from jax.experimental.pallas import tpu as pltpu
from jax.sharding import Mesh
from jax.sharding import PartitionSpec as P

STATE = ("state_0", "state_1")
ROW = "bond_0"
FAR = "bond_1"
NEAR = "bond_2"
CORE = "bond_3"


ORDER = (0, 7, 1, 6, 2, 5, 3, 4)


def shifted(value, axis, step):
    size = lax.axis_size(axis)
    return lax.ppermute(value, axis, [(i, (i + step) % size) for i in range(size)])


def exchanged(value, axis):
    return lax.all_to_all(value, axis, split_axis=0, concat_axis=0, tiled=True)


def sent_to_all(value, axis):
    return exchanged(jnp.broadcast_to(value, (lax.axis_size(axis), *value.shape)), axis)


def rows_times(left, right):
    return lax.dot_general(left, right, (((1,), (1,)), ((), ())), preferred_element_type=jnp.float32)


def paired(pieces):
    for step in range(0, len(ORDER), 2):
        left = jnp.concatenate([piece[...] for piece in pieces[step : step + 2]])
        yield left, ORDER[step : step + 2]


def join_kernel(*refs):
    *pieces, out = refs
    for k, piece in enumerate(pieces):
        out[k] = piece[...]


def joined(*pieces):
    resident = pl.BlockSpec(memory_space=pltpu.VMEM)
    return pl.pallas_call(
        join_kernel,
        out_shape=jax.ShapeDtypeStruct((len(pieces), *pieces[0].shape), pieces[0].dtype),
        in_specs=[resident] * len(pieces),
        out_specs=resident,
    )(*pieces)


def project_kernel(*refs):
    pieces = refs[:8]
    stored = refs[8:10]
    spread, out = refs[10:]
    z = lax.axis_index(ROW)
    v = lax.axis_index(NEAR)
    c = lax.axis_index(CORE)
    height, count = spread.shape[3:]
    rows, slots = out.shape[:2]
    wide = spread.shape[0]
    behind = spread.shape[2] - slots
    right = jnp.concatenate([piece[...] for piece in stored])
    targets = [
        lax.rem(v + flip_v, 2) * 2 + lax.rem(c + flip_c, 2)
        for flip_v, flip_c in ((0, 0), (1, 0), (0, 1), (1, 1))
    ]
    total = jnp.zeros((height, count), jnp.float32)
    for left, offsets in paired(pieces):
        product = rows_times(left, right)
        for i, offset in enumerate(offsets):
            place = lax.rem(z + offset, rows)
            for k, target in enumerate(targets):
                one = product[i * height : (i + 1) * height, k * count : (k + 1) * count]
                out[place, target, :height] = one.astype(jnp.bfloat16)
                current = spread[lax.rem(place, wide), place // wide, behind + target]
                total += one * current.astype(jnp.float32)
    whole = jnp.full((8, count), jnp.sum(total), jnp.float32)
    high = whole.astype(jnp.bfloat16).astype(jnp.float32)
    middle = (whole - high).astype(jnp.bfloat16).astype(jnp.float32)
    low = whole - high - middle
    row = lax.broadcasted_iota(jnp.int32, whole.shape, 0)
    parts = jnp.where(row == 0, high, jnp.where(row == 1, middle, jnp.where(row == 2, low, 0.0)))
    for i in range(rows):
        for k in range(slots):
            out[i, k, height:] = parts.astype(jnp.bfloat16)


def grow_kernel(*refs):
    pieces = refs[:8]
    mine, other, spread, keep, give, operand, moved, semaphores = refs[8:]
    z = lax.axis_index(ROW)
    y = lax.axis_index(FAR) * 2 + lax.axis_index(NEAR)
    c = lax.axis_index(CORE)
    copies = []
    for k, offset in enumerate((0, 3, 1, 2)):
        for flip, source in enumerate((mine, other)):
            slot = lax.rem(y + offset, 4) * 2 + lax.rem(c + flip, 2)
            for s in range(operand.shape[0]):
                copy = pltpu.make_async_copy(
                    source.at[k, s], operand.at[s, slot], semaphores.at[len(copies)]
                )
                copy.start()
                copies.append(copy)
    for copy in copies:
        copy.wait()
    physical, slots, count, bond = operand.shape
    block = slots * count
    height, half = spread.shape[3:]
    rows = moved.shape[0]
    wide = spread.shape[0]
    right = operand[...].reshape(physical * block, bond)
    for left, offsets in paired(pieces):
        product = rows_times(left, right).astype(jnp.bfloat16)
        for i, offset in enumerate(offsets):
            moved[lax.rem(z + offset, rows)] = product[i * height : (i + 1) * height]
    inner = moved[...].reshape(rows * height, physical * block)
    for k in range(keep.shape[0]):
        total = jnp.zeros((half, block), jnp.float32)
        for s in range(physical):
            left = spread[k % wide, k // wide, s * rows : (s + 1) * rows]
            total += lax.dot_general(
                left.reshape(rows * height, half),
                inner[:, s * block : (s + 1) * block],
                (((0,), (0,)), ((), ())),
                preferred_element_type=jnp.float32,
            )
        for i in range(2):
            first = total[2 * i * count : (2 * i + 1) * count]
            second = total[(2 * i + 1) * count : (2 * i + 2) * count]
            keep[k, i] = jnp.where(c == 0, first, second).astype(jnp.bfloat16)
            give[k, i] = jnp.where(c == 0, second, first).astype(jnp.bfloat16)


def whole(intersect_left, stored_block, stored_site, current_site, current_block, penalty_weight):
    states = lax.axis_size(STATE)
    rows = lax.axis_size(ROW)
    pairs, width, bond = stored_block.shape[1:]
    physical = stored_site.shape[1]
    block = current_block.shape[2]
    slots = 4
    count = pairs * width
    height = 2 * width
    half = block // 2
    group = (*STATE, NEAR, CORE)
    anywhere = pl.BlockSpec(memory_space=pl.ANY)
    resident = pl.BlockSpec(memory_space=pltpu.VMEM)

    both = jnp.concatenate(
        [current_block.reshape(count, block), current_site.reshape(width * physical, block)]
    )
    across = shifted(both, STATE[0], 1)
    low = lax.axis_index(STATE[0]) == 0
    both = jnp.where(low, jnp.stack([both, across]), jnp.stack([across, both]))

    turned = both[:, :count].transpose(0, 2, 1).reshape(2, 2, slots, width, count)
    turned = turned.transpose(2, 0, 1, 3, 4).reshape(slots, 2, height, count)
    current = exchanged(turned, (NEAR, CORE)).transpose(1, 0, 2, 3)

    first = lax.axis_index(FAR) == 0
    mine = intersect_left[0]
    site = both[:, count:].reshape(2, width, physical, block).transpose(1, 0, 2, 3)
    site = site.reshape(width, 2 * physical, block)
    kept = jnp.where(first, site[:, :, :half], site[:, :, half:]).reshape(width, -1)
    given = jnp.where(first, site[:, :, half:], site[:, :, :half]).reshape(width, -1)
    other = shifted(jnp.concatenate([mine, given], axis=1), FAR, 1)
    got = other[:, bond:]
    other = other[:, :bond]
    site = jnp.where(first, jnp.stack([kept, got]), jnp.stack([got, kept]))
    site = site.reshape(height, 2 * physical, half).transpose(1, 0, 2)
    site = sent_to_all(site, ROW)
    site = site.transpose(1, 0, 2, 3).reshape(2, physical * rows, height, half)
    spread = sent_to_all(jnp.concatenate([site, current], axis=1), STATE[1])
    environment = jnp.where(first, jnp.stack([mine, other]), jnp.stack([other, mine]))
    environment = environment.reshape(height, bond)
    pieces = [environment]
    below = above = environment
    for _ in range(1, rows // 2):
        below = shifted(below, ROW, 1)
        above = shifted(above, ROW, -1)
        pieces += [below, above]
    pieces.append(shifted(below, ROW, 1))

    column = (FAR, NEAR)
    local = stored_site[0].reshape(physical * width, bond)
    left = shifted(local, column, 1)
    right = shifted(local, column, -1)
    opposite = shifted(local, FAR, 1)
    local = joined(local, left, right, opposite)
    across = shifted(local, CORE, 1)
    local = local.reshape(4, physical, width, bond)
    across = across.reshape(4, physical, width, bond)

    stored = stored_block[0].reshape(count, bond)
    stored_near = shifted(stored, NEAR, 1)
    stored_pair = joined(stored, stored_near).reshape(2 * count, bond)
    stored_other = shifted(stored_pair, CORE, 1)

    projected = pl.pallas_call(
        project_kernel,
        out_shape=jax.ShapeDtypeStruct((rows, slots, height + 8, count), jnp.bfloat16),
        in_specs=[resident] * 11,
        out_specs=resident,
        cost_estimate=pl.CostEstimate(flops=2 * 512 * 512 * 2048, bytes_accessed=5 << 20, transcendentals=0),
        name="project",
    )(*pieces, stored_pair, stored_other, spread)


    received = exchanged(projected.reshape(-1, height + 8, count), group)
    received = received.reshape(states, slots, height + 8, count).astype(jnp.float32)
    total = received[:, :, height : height + 3].sum(axis=(1, 2))
    total = total + shifted(total, FAR, 1)

    keep, give = pl.pallas_call(
        grow_kernel,
        out_shape=(jax.ShapeDtypeStruct((states, 2, width, block), jnp.bfloat16),) * 2,
        in_specs=[resident] * 8 + [anywhere] * 2 + [resident],
        out_specs=(resident, resident),
        scratch_shapes=[
            pltpu.VMEM((physical, 8, width, bond), jnp.bfloat16),
            pltpu.VMEM((rows, height, physical * block), jnp.bfloat16),
            pltpu.SemaphoreType.DMA((16,)),
        ],
        cost_estimate=pl.CostEstimate(flops=3 * 512 * 512 * 2048, bytes_accessed=6 << 20, transcendentals=0),
        name="grow",
    )(*pieces, local, across, spread)
    got = shifted(give, CORE, 1)
    grown = (keep.astype(jnp.float32) + got.astype(jnp.float32)).astype(jnp.bfloat16)

    total = jnp.broadcast_to(total[:, :1], (states, block))
    high = lax.reduce_precision(total, 8, 7)
    middle = lax.reduce_precision(total - high, 8, 7)
    low = total - high - middle
    lane = lax.broadcasted_iota(jnp.int32, total.shape, 1)
    parts = jnp.where(lane == 0, high, jnp.where(lane == 1, middle, jnp.where(lane == 2, low, 0.0)))
    parts = parts.astype(jnp.bfloat16)[:, None]
    parts = jnp.broadcast_to(parts.reshape(1, 1, states, block), (states, 2, 8, block))
    grown = jnp.concatenate([grown, parts], axis=2).reshape(states * 2, width + 8, block)
    grown = exchanged(grown, (ROW, NEAR))
    grown = grown.reshape(rows, 2, width + 8, block).astype(jnp.float32)
    intersect = grown[:, 0, width:, :3].sum(axis=(0, 2)) * (1.0 / (physical * bond))
    grown = grown[:, :, :width].sum(axis=1)
    intersect_next = grown.astype(jnp.bfloat16).transpose(1, 0, 2).reshape(1, width, rows * block)

    gain = penalty_weight * intersect
    summed = jnp.sum(gain[:, None, None, None] * received[:, :, :height], axis=0)
    summed = summed.reshape(slots, 2, width, count).transpose(1, 0, 2, 3).reshape(block, count)
    penalized = current_block.astype(jnp.float32) + summed.T.reshape(pairs, width, block)
    return (penalized, intersect_next)


def solution(mesh):
    torus = Mesh(
        mesh.devices.reshape(2, mesh.shape["state"] // 2, 8, 2, 2, 2),
        (*STATE, ROW, FAR, NEAR, CORE),
    )
    bond = (ROW, FAR, NEAR, CORE)
    in_specs = (
        P(STATE, bond, None),
        P(STATE, None, bond, None),
        P(STATE, None, bond, None),
        P(bond, None, STATE),
        P(None, bond, STATE),
        P(),
    )
    out_specs = (P(None, bond, STATE), P(STATE, bond, None))
    return jax.shard_map(whole, mesh=torus, in_specs=in_specs, out_specs=out_specs, check_vma=False)
```

time: 238 us -> 206 us (0.87)
  the two profiles are of different devices: /device:TPU:63 before, /device:TPU:1 now
where the time goes in v1:
time: 206 us; the launch traced here: 202 us
  starting transfers between devices  83.7 us (41%)
  waiting for transfers between devices  73.4 us (36%)
  Pallas kernels  19.8 us (10%)
  blocking collectives  13.8 us (7%)
  local copies, waits for them, and re-layouts  7.99 us (4%)
  other arithmetic  2.33 us (1%)
    ppermute x17, starting transfers between devices, shifted(): lax.ppermute(value, axis, [(i, (i + step) % size) for i in range(size)])  53.5 us
    ppermute x17, waiting for transfers between devices, shifted(): lax.ppermute(value, axis, [(i, (i + step) % size) for i in range(size)])  41.4 us
    all_to_all x4, waiting for transfers between devices, exchanged(): return lax.all_to_all(value, axis, split_axis=0, concat_axis=0, tiled=True)  32 us
    all_to_all x4, starting transfers between devices, exchanged(): return lax.all_to_all(value, axis, split_axis=0, concat_axis=0, tiled=True)  30.2 us
    all_to_all x1, blocking collectives, exchanged(): return lax.all_to_all(value, axis, split_axis=0, concat_axis=0, tiled=True)  13.8 us
    pallas_call x1, Pallas kernels, whole(): pl.pallas_call(grow_kernel, out_shape=(jax.ShapeDtypeStruct((states, 2, w...  8.53 us
    pallas_call x1, Pallas kernels, whole(): pl.pallas_call(project_kernel, out_shape=jax.ShapeDtypeStruct((rows, slot...  6.79 us
    pallas_call x2, Pallas kernels, joined(): pl.pallas_call(join_kernel, out_shape=jax.ShapeDtypeStruct((len(pieces),...  4.5 us
  transfers between devices with their start and end apart: 21, of which 9 were waited for; matrix products, arithmetic and copies ran while one was open for 1% of the time, Pallas kernels for 10%

profile of v1, /device:TPU:1, one launch (start us, length us, event | category | flops | bytes accessed | tf_op | source)
XLA Modules:
  0.0 202.3 jit_solution(9756365016042249068)
XLA Ops:
  2.3 4.0 %collective-permute-start = (bf16[192,256]{1,0:T(8,128)(2,1)S(1)}, bf16[192,256]{1,0:T(8,128)(2,1)S(1)}, u32[]{:S(2)}, u32[]{:S(2)}) collective-permute-start(bf16[192,256]{1,0:T(8,128)(2,1)S(1)} %get-tuple-element.7), channel_id=1, source_target_pairs={{0,256},{256,0},{1,257},{257,1},{2,258},{258,2},{3,259},{259,3},{4... | collective-permute-start | bytes 294920 | tf_op jit(solution)/shard_map/ppermute | solution.py:21
  8.5 7.6 %collective-permute-start.1 = (bf16[32,2560]{1,0:T(8,128)(2,1)S(1)}, bf16[32,2560]{1,0:T(8,128)(2,1)S(1)}, u32[]{:S(2)}, u32[]{:S(2)}) collective-permute-start(bf16[32,2560]{1,0:T(8,128)(2,1)S(1)} %pad_maximum_fusion.2), channel_id=1, source_target_pairs={{0,4},{4,0},{1,5},{5,1},{2,6},{6,2},{3,7},{7,3},{8,12},{12,8},{9,1... | collective-permute-start | bytes 491528 | tf_op jit(solution)/shard_map/ppermute | solution.py:21
  17.0 5.4 %all-to-all-start.1 = ((bf16[4,2,64,128]{3,2,1,0:T(8,128)(2,1)}), bf16[4,2,64,128]{3,2,1,0:T(8,128)(2,1)S(1)}, u32[]{:S(2)}, u32[]{:S(2)}) async-start(bf16[4,2,64,128]{3,2,1,0:T(8,128)(2,1)} %bitcast.19), calls=%async_computation.1 | async-start | bytes 262144 | tf_op jit(solution)/shard_map/all_to_all | solution.py:25
  22.5 7.6 %all-to-all-done.1 = bf16[4,2,64,128]{3,2,1,0:T(8,128)(2,1)S(1)} async-done(((bf16[4,2,64,128]{3,2,1,0:T(8,128)(2,1)}), bf16[4,2,64,128]{3,2,1,0:T(8,128)(2,1)S(1)}, u32[]{:S(2)}, u32[]{:S(2)}) %all-to-all-start.1) | async-done | bytes 131104 | tf_op jit(solution)/shard_map/all_to_all | solution.py:25
  31.0 8.7 %all-to-all-start = ((bf16[8,4,64,128]{3,2,1,0:T(8,128)(2,1)}), bf16[8,4,64,128]{3,2,1,0:T(8,128)(2,1)S(1)}, u32[]{:S(2)}, u32[]{:S(2)}) async-start(bf16[8,4,64,128]{3,2,1,0:T(8,128)(2,1)} %broadcast_in_dim.27), calls=%async_computation | async-start | bytes 1048576 | tf_op jit(solution)/shard_map/all_to_all | solution.py:25
  39.7 17.9 %all-to-all-done = bf16[8,4,64,128]{3,2,1,0:T(8,128)(2,1)S(1)} async-done(((bf16[8,4,64,128]{3,2,1,0:T(8,128)(2,1)}), bf16[8,4,64,128]{3,2,1,0:T(8,128)(2,1)S(1)}, u32[]{:S(2)}, u32[]{:S(2)}) %all-to-all-start) | async-done | bytes 524320 | tf_op jit(solution)/shard_map/all_to_all | solution.py:25
  59.9 4.0 %all-to-all-start.2 = ((bf16[4,2,20,64,128]{4,3,2,1,0:T(8,128)(2,1)}), bf16[4,2,20,64,128]{4,3,2,1,0:T(8,128)(2,1)S(1)}, u32[]{:S(2)}, u32[]{:S(2)}) async-start(bf16[4,2,20,64,128]{4,3,2,1,0:T(8,128)(2,1)} %broadcast_in_dim.28), calls=%async_computation.2 | async-start | bytes 5242880 | tf_op jit(solution)/shard_map/all_to_all | solution.py:25
  67.8 23.8 %collective-permute-done.14.refs_1_ = bf16[128,2048]{1,0:T(8,128)(2,1)} collective-permute-done((bf16[128,2048]{1,0:T(8,128)(2,1)}, bf16[128,2048]{1,0:T(8,128)(2,1)}, u32[]{:S(2)}, u32[]{:S(2)}) %collective-permute-start.14) | collective-permute-done | bytes 524320 | tf_op jit(solution)/shard_map/ppermute | solution.py:21
  93.9 2.4 %collective-permute-start.15 = (bf16[256,2048]{1,0:T(8,128)(2,1)}, bf16[256,2048]{1,0:T(8,128)(2,1)}, u32[]{:S(2)}, u32[]{:S(2)}) collective-permute-start(bf16[256,2048]{1,0:T(8,128)(2,1)} %bitcast.55), channel_id=1, source_target_pairs={{0,1},{1,0},{2,3},{3,2},{4,5},{5,4},{6,7},{7,6},{8,9},{9,8},{10,11... | collective-permute-start | bytes 3145736 | tf_op jit(solution)/shard_map/ppermute | solution.py:21
  98.3 3.4 %collective-permute-start.4 = (bf16[64,2048]{1,0:T(8,128)(2,1)S(1)}, bf16[64,2048]{1,0:T(8,128)(2,1)S(1)}, u32[]{:S(2)}, u32[]{:S(2)}) collective-permute-start(bf16[64,2048]{1,0:T(8,128)(2,1)S(1)} %collective-permute-done.2.refs_1_), channel_id=1, source_target_pairs={{0,8},{8,16},{16,24},{24,32},{32,40},{40,48},{48,56},{56,0},{1,9},... | collective-permute-start | bytes 786440 | tf_op jit(solution)/shard_map/ppermute | solution.py:21
  103.6 2.5 %collective-permute-done.3.refs_2_ = bf16[64,2048]{1,0:T(8,128)(2,1)S(1)} collective-permute-done((bf16[64,2048]{1,0:T(8,128)(2,1)S(1)}, bf16[64,2048]{1,0:T(8,128)(2,1)S(1)}, u32[]{:S(2)}, u32[]{:S(2)}) %collective-permute-start.3) | collective-permute-done | bytes 262176 | tf_op jit(solution)/shard_map/ppermute | solution.py:21
  106.1 3.4 %collective-permute-start.5 = (bf16[64,2048]{1,0:T(8,128)(2,1)S(1)}, bf16[64,2048]{1,0:T(8,128)(2,1)}, u32[]{:S(2)}, u32[]{:S(2)}) collective-permute-start(bf16[64,2048]{1,0:T(8,128)(2,1)S(1)} %collective-permute-done.3.refs_2_), channel_id=1, source_target_pairs={{0,56},{8,0},{16,8},{24,16},{32,24},{40,32},{48,40},{56,48},{1,57}... | collective-permute-start | bytes 786440 | tf_op jit(solution)/shard_map/ppermute | solution.py:21
  111.4 3.9 %collective-permute-start.11 = (bf16[64,2048]{1,0:T(8,128)(2,1)}, bf16[64,2048]{1,0:T(8,128)(2,1)}, u32[]{:S(2)}, u32[]{:S(2)}) collective-permute-start(bf16[64,2048]{1,0:T(8,128)(2,1)} %bitcast.77), channel_id=1, source_target_pairs={{0,4},{4,0},{1,5},{5,1},{2,6},{6,2},{3,7},{7,3},{8,12},{12,8},{9,1... | collective-permute-start | bytes 786440 | tf_op jit(solution)/shard_map/ppermute | solution.py:21
  117.3 4.6 %collective-permute-start.7 = (bf16[64,2048]{1,0:T(8,128)(2,1)}, bf16[64,2048]{1,0:T(8,128)(2,1)}, u32[]{:S(2)}, u32[]{:S(2)}) collective-permute-start(bf16[64,2048]{1,0:T(8,128)(2,1)} %collective-permute-done.5.refs_4_), channel_id=1, source_target_pairs={{0,56},{8,0},{16,8},{24,16},{32,24},{40,32},{48,40},{56,48},{1,57}... | collective-permute-start | bytes 786440 | tf_op jit(solution)/shard_map/ppermute | solution.py:21
  123.8 7.2 %collective-permute-done.11.refs_3_ = bf16[64,2048]{1,0:T(8,128)(2,1)} collective-permute-done((bf16[64,2048]{1,0:T(8,128)(2,1)}, bf16[64,2048]{1,0:T(8,128)(2,1)}, u32[]{:S(2)}, u32[]{:S(2)}) %collective-permute-start.11) | collective-permute-done | bytes 262176 | tf_op jit(solution)/shard_map/ppermute | solution.py:21
  131.0 2.5 %collective-permute-done.9.refs_1_ = bf16[64,2048]{1,0:T(8,128)(2,1)} collective-permute-done((bf16[64,2048]{1,0:T(8,128)(2,1)}, bf16[64,2048]{1,0:T(8,128)(2,1)}, u32[]{:S(2)}, u32[]{:S(2)}) %collective-permute-start.9) | collective-permute-done | bytes 262176 | tf_op jit(solution)/shard_map/ppermute | solution.py:21
  135.7 3.8 %collective-permute-start.12 = (bf16[4,64,2048]{2,1,0:T(8,128)(2,1)}, bf16[4,64,2048]{2,1,0:T(8,128)(2,1)}, u32[]{:S(2)}, u32[]{:S(2)}) collective-permute-start(bf16[4,64,2048]{2,1,0:T(8,128)(2,1)} %shard_map.77), channel_id=1, source_target_pairs={{0,1},{1,0},{2,3},{3,2},{4,5},{5,4},{6,7},{7,6},{8,9},{9,8},{10,11... | collective-permute-start | bytes 3145736 | tf_op jit(solution)/shard_map/ppermute | solution.py:21
  141.1 6.8 %project.1 = bf16[8,4,72,128]{3,2,1,0:T(8,128)(2,1)} custom-call(bf16[64,2048]{1,0:T(8,128)(2,1)} %bitcast.61, bf16[64,2048]{1,0:T(8,128)(2,1)} %copy-done.2, bf16[64,2048]{1,0:T(8,128)(2,1)} %copy-done.3, bf16[64,2048]{1,0:T(8,128)(2,1)} %copy-done.4, bf16[64,2048]{1,0:T(8,128)(2,1)} %collective-permute-done.5.refs_4_, ...), custom_call_target="tpu_custom_call" | custom-call | flops 1073741824 | bytes 5242880 | tf_op jit(solution)/shard_map/project/pallas_call | solution.py:205
  147.9 12.1 %all-to-all-start.3 = ((bf16[32,72,128]{2,1,0:T(8,128)(2,1)}), bf16[32,72,128]{2,1,0:T(8,128)(2,1)S(1)}, u32[]{:S(2)}, u32[]{:S(2)}) async-start(bf16[32,72,128]{2,1,0:T(8,128)(2,1)} %bitcast.58), calls=%async_computation.3 | async-start | bytes 1179648 | tf_op jit(solution)/shard_map/all_to_all | solution.py:25
  160.1 8.5 %grow.1 = (bf16[8,2,32,256]{3,2,1,0:T(8,128)(2,1)}, bf16[8,2,32,256]{3,2,1,0:T(8,128)(2,1)}) custom-call(bf16[64,2048]{1,0:T(8,128)(2,1)} %bitcast.62, bf16[64,2048]{1,0:T(8,128)(2,1)} %copy-done.2, bf16[64,2048]{1,0:T(8,128)(2,1)} %copy-done.3, bf16[64,2048]{1,0:T(8,128)(2,1)} %copy-done.4, bf16[64,2048]{1,0:T(8,128)(2,1)} %collective-permute-done.5.refs_4_, ...), custom_call_target="tpu_custom_call" | custom-call | flops 1610612736 | bytes 6291456 | tf_op jit(solution)/shard_map/grow/pallas_call | solution.py:220
  170.9 6.5 %all-to-all-done.3 = bf16[32,72,128]{2,1,0:T(8,128)(2,1)S(1)} async-done(((bf16[32,72,128]{2,1,0:T(8,128)(2,1)}), bf16[32,72,128]{2,1,0:T(8,128)(2,1)S(1)}, u32[]{:S(2)}, u32[]{:S(2)}) %all-to-all-start.3) | async-done | bytes 589856 | tf_op jit(solution)/shard_map/all_to_all | solution.py:25
  177.5 4.7 %collective-permute-start.16 = (f32[8,128]{1,0:T(8,128)S(1)}, f32[8,128]{1,0:T(8,128)S(1)}, u32[]{:S(2)}, u32[]{:S(2)}) collective-permute-start(f32[8,128]{1,0:T(8,128)S(1)} %slice_reduce_fusion.1), channel_id=1, source_target_pairs={{0,4},{4,0},{1,5},{5,1},{2,6},{6,2},{3,7},{7,3},{8,12},{12,8},{9,1... | collective-permute-start | bytes 12296 | tf_op jit(solution)/shard_map/ppermute | solution.py:21
  182.3 3.4 %collective-permute-done.16 = f32[8,128]{1,0:T(8,128)S(1)} collective-permute-done((f32[8,128]{1,0:T(8,128)S(1)}, f32[8,128]{1,0:T(8,128)S(1)}, u32[]{:S(2)}, u32[]{:S(2)}) %collective-permute-start.16) | collective-permute-done | bytes 4128 | tf_op jit(solution)/shard_map/ppermute | solution.py:21
  186.0 13.8 %all_to_all.25 = bf16[16,40,256]{2,1,0:T(8,128)(2,1)S(1)} all-to-all(bf16[16,40,256]{2,1,0:T(8,128)(2,1)S(1)} %bitcast.64), channel_id=1, replica_groups=mesh['state_0'=2,'state_1'=4,'bond_0'=8,'bond_1'=2,'bond_2'=2,'bond_3'=2..., dimensions={0} | all-to-all | bytes 655360 | tf_op jit(solution)/shard_map/all_to_all | solution.py:25
  (89 shorter events, 32.6 us)
Async XLA Ops:
  2.3 6.0 %collective-permute-start = (bf16[192,256]{1,0:T(8,128)(2,1)S(1)}, bf16[192,256]{1,0:T(8,128)(2,1)S(1)}, u32[]{:S(2)}, u32[]{:S(2)}) collective-permute-start(bf16[192,256]{1,0:T(8,128)(2,1)S(1)} %get-tuple-element.7), channel_id=1, source_target_pairs={{0,256},{256,0},{1,257},{257,1},{2,258},{258,2},{3,259},{259,3},{4... | collective-permute-start | bytes 294920 | tf_op jit(solution)/shard_map/ppermute | solution.py:21
  8.5 13.9 %collective-permute-start.1 = (bf16[32,2560]{1,0:T(8,128)(2,1)S(1)}, bf16[32,2560]{1,0:T(8,128)(2,1)S(1)}, u32[]{:S(2)}, u32[]{:S(2)}) collective-permute-start(bf16[32,2560]{1,0:T(8,128)(2,1)S(1)} %pad_maximum_fusion.2), channel_id=1, source_target_pairs={{0,4},{4,0},{1,5},{5,1},{2,6},{6,2},{3,7},{7,3},{8,12},{12,8},{9,1... | collective-permute-start | bytes 491528 | tf_op jit(solution)/shard_map/ppermute | solution.py:21
  17.0 13.0 %all-to-all-start.1 = ((bf16[4,2,64,128]{3,2,1,0:T(8,128)(2,1)}), bf16[4,2,64,128]{3,2,1,0:T(8,128)(2,1)S(1)}, u32[]{:S(2)}, u32[]{:S(2)}) async-start(bf16[4,2,64,128]{3,2,1,0:T(8,128)(2,1)} %bitcast.19), calls=%async_computation.1 | async-start | bytes 262144 | tf_op jit(solution)/shard_map/all_to_all | solution.py:25
  31.0 26.6 %all-to-all-start = ((bf16[8,4,64,128]{3,2,1,0:T(8,128)(2,1)}), bf16[8,4,64,128]{3,2,1,0:T(8,128)(2,1)S(1)}, u32[]{:S(2)}, u32[]{:S(2)}) async-start(bf16[8,4,64,128]{3,2,1,0:T(8,128)(2,1)} %broadcast_in_dim.27), calls=%async_computation | async-start | bytes 1048576 | tf_op jit(solution)/shard_map/all_to_all | solution.py:25
  59.9 79.7 %all-to-all-start.2 = ((bf16[4,2,20,64,128]{4,3,2,1,0:T(8,128)(2,1)}), bf16[4,2,20,64,128]{4,3,2,1,0:T(8,128)(2,1)S(1)}, u32[]{:S(2)}, u32[]{:S(2)}) async-start(bf16[4,2,20,64,128]{4,3,2,1,0:T(8,128)(2,1)} %broadcast_in_dim.28), calls=%async_computation.2 | async-start | bytes 5242880 | tf_op jit(solution)/shard_map/all_to_all | solution.py:25
  63.9 27.7 %collective-permute-start.14 = (bf16[128,2048]{1,0:T(8,128)(2,1)}, bf16[128,2048]{1,0:T(8,128)(2,1)}, u32[]{:S(2)}, u32[]{:S(2)}) collective-permute-start(bf16[128,2048]{1,0:T(8,128)(2,1)} %bitcast.21.refs_0_), channel_id=1, source_target_pairs={{0,2},{2,0},{1,3},{3,1},{4,6},{6,4},{5,7},{7,5},{8,10},{10,8},{9,1... | collective-permute-start | bytes 1572872 | tf_op jit(solution)/shard_map/ppermute | solution.py:21
  65.9 69.9 %copy-start.1 = (bf16[2,32,2048]{2,1,0:T(8,128)(2,1)}, bf16[2,32,2048]{2,1,0:T(8,128)(2,1)S(1)}, u32[]{:S(2)}) copy-start(bf16[2,32,2048]{2,1,0:T(8,128)(2,1)S(1)} %maximum_select_fusion) | copy-start | bytes 786436
  65.9 32.3 %collective-permute-start.2 = (bf16[64,2048]{1,0:T(8,128)(2,1)S(1)}, bf16[64,2048]{1,0:T(8,128)(2,1)S(1)}, u32[]{:S(2)}, u32[]{:S(2)}) collective-permute-start(bf16[64,2048]{1,0:T(8,128)(2,1)S(1)} %bitcast.59), channel_id=1, source_target_pairs={{0,8},{8,16},{16,24},{24,32},{32,40},{40,48},{48,56},{56,0},{1,9},... | collective-permute-start | bytes 786440 | tf_op jit(solution)/shard_map/ppermute | solution.py:21
  93.9 45.7 %collective-permute-start.15 = (bf16[256,2048]{1,0:T(8,128)(2,1)}, bf16[256,2048]{1,0:T(8,128)(2,1)}, u32[]{:S(2)}, u32[]{:S(2)}) collective-permute-start(bf16[256,2048]{1,0:T(8,128)(2,1)} %bitcast.55), channel_id=1, source_target_pairs={{0,1},{1,0},{2,3},{3,2},{4,5},{5,4},{6,7},{7,6},{8,9},{9,8},{10,11... | collective-permute-start | bytes 3145736 | tf_op jit(solution)/shard_map/ppermute | solution.py:21
  96.3 9.7 %collective-permute-start.3 = (bf16[64,2048]{1,0:T(8,128)(2,1)S(1)}, bf16[64,2048]{1,0:T(8,128)(2,1)S(1)}, u32[]{:S(2)}, u32[]{:S(2)}) collective-permute-start(bf16[64,2048]{1,0:T(8,128)(2,1)S(1)} %bitcast.60), channel_id=1, source_target_pairs={{0,56},{8,0},{16,8},{24,16},{32,24},{40,32},{48,40},{56,48},{1,57}... | collective-permute-start | bytes 786440 | tf_op jit(solution)/shard_map/ppermute | solution.py:21
  98.2 41.3 %copy-start.2 = (bf16[64,2048]{1,0:T(8,128)(2,1)}, bf16[64,2048]{1,0:T(8,128)(2,1)S(1)}, u32[]{:S(2)}) copy-start(bf16[64,2048]{1,0:T(8,128)(2,1)S(1)} %collective-permute-done.2.refs_1_) | copy-start | bytes 786436
  98.3 11.2 %collective-permute-start.4 = (bf16[64,2048]{1,0:T(8,128)(2,1)S(1)}, bf16[64,2048]{1,0:T(8,128)(2,1)S(1)}, u32[]{:S(2)}, u32[]{:S(2)}) collective-permute-start(bf16[64,2048]{1,0:T(8,128)(2,1)S(1)} %collective-permute-done.2.refs_1_), channel_id=1, source_target_pairs={{0,8},{8,16},{16,24},{24,32},{32,40},{40,48},{48,56},{56,0},{1,9},... | collective-permute-start | bytes 786440 | tf_op jit(solution)/shard_map/ppermute | solution.py:21
  101.6 13.7 %collective-permute-start.10 = (bf16[64,2048]{1,0:T(8,128)(2,1)}, bf16[64,2048]{1,0:T(8,128)(2,1)S(1)}, u32[]{:S(2)}, u32[]{:S(2)}) collective-permute-start(bf16[64,2048]{1,0:T(8,128)(2,1)} %bitcast.76), channel_id=1, source_target_pairs={{0,6},{2,0},{4,2},{6,4},{1,7},{3,1},{5,3},{7,5},{8,14},{10,8},{12,... | collective-permute-start | bytes 786440 | tf_op jit(solution)/shard_map/ppermute | solution.py:21
  106.1 33.6 %copy-start.3 = (bf16[64,2048]{1,0:T(8,128)(2,1)}, bf16[64,2048]{1,0:T(8,128)(2,1)S(1)}, u32[]{:S(2)}) copy-start(bf16[64,2048]{1,0:T(8,128)(2,1)S(1)} %collective-permute-done.3.refs_2_) | copy-start | bytes 786436
  106.1 11.2 %collective-permute-start.5 = (bf16[64,2048]{1,0:T(8,128)(2,1)S(1)}, bf16[64,2048]{1,0:T(8,128)(2,1)}, u32[]{:S(2)}, u32[]{:S(2)}) collective-permute-start(bf16[64,2048]{1,0:T(8,128)(2,1)S(1)} %collective-permute-done.3.refs_2_), channel_id=1, source_target_pairs={{0,56},{8,0},{16,8},{24,16},{32,24},{40,32},{48,40},{56,48},{1,57}... | collective-permute-start | bytes 786440 | tf_op jit(solution)/shard_map/ppermute | solution.py:21
  109.5 12.4 %collective-permute-start.6 = (bf16[64,2048]{1,0:T(8,128)(2,1)S(1)}, bf16[64,2048]{1,0:T(8,128)(2,1)}, u32[]{:S(2)}, u32[]{:S(2)}) collective-permute-start(bf16[64,2048]{1,0:T(8,128)(2,1)S(1)} %collective-permute-done.4.refs_3_), channel_id=1, source_target_pairs={{0,8},{8,16},{16,24},{24,32},{32,40},{40,48},{48,56},{56,0},{1,9},... | collective-permute-start | bytes 786440 | tf_op jit(solution)/shard_map/ppermute | solution.py:21
  111.4 19.5 %collective-permute-start.11 = (bf16[64,2048]{1,0:T(8,128)(2,1)}, bf16[64,2048]{1,0:T(8,128)(2,1)}, u32[]{:S(2)}, u32[]{:S(2)}) collective-permute-start(bf16[64,2048]{1,0:T(8,128)(2,1)} %bitcast.77), channel_id=1, source_target_pairs={{0,4},{4,0},{1,5},{5,1},{2,6},{6,2},{3,7},{7,3},{8,12},{12,8},{9,1... | collective-permute-start | bytes 786440 | tf_op jit(solution)/shard_map/ppermute | solution.py:21
  115.3 18.2 %collective-permute-start.9 = (bf16[64,2048]{1,0:T(8,128)(2,1)}, bf16[64,2048]{1,0:T(8,128)(2,1)}, u32[]{:S(2)}, u32[]{:S(2)}) collective-permute-start(bf16[64,2048]{1,0:T(8,128)(2,1)} %bitcast.78), channel_id=1, source_target_pairs={{0,2},{2,4},{4,6},{6,0},{1,3},{3,5},{5,7},{7,1},{8,10},{10,12},{12... | collective-permute-start | bytes 786440 | tf_op jit(solution)/shard_map/ppermute | solution.py:21
  117.3 22.3 %collective-permute-start.7 = (bf16[64,2048]{1,0:T(8,128)(2,1)}, bf16[64,2048]{1,0:T(8,128)(2,1)}, u32[]{:S(2)}, u32[]{:S(2)}) collective-permute-start(bf16[64,2048]{1,0:T(8,128)(2,1)} %collective-permute-done.5.refs_4_), channel_id=1, source_target_pairs={{0,56},{8,0},{16,8},{24,16},{32,24},{40,32},{48,40},{56,48},{1,57}... | collective-permute-start | bytes 786440 | tf_op jit(solution)/shard_map/ppermute | solution.py:21
  121.9 17.7 %collective-permute-start.8 = (bf16[64,2048]{1,0:T(8,128)(2,1)}, bf16[64,2048]{1,0:T(8,128)(2,1)}, u32[]{:S(2)}, u32[]{:S(2)}) collective-permute-start(bf16[64,2048]{1,0:T(8,128)(2,1)} %collective-permute-done.6.refs_5_), channel_id=1, source_target_pairs={{0,8},{8,16},{16,24},{24,32},{32,40},{40,48},{48,56},{56,0},{1,9},... | collective-permute-start | bytes 786440 | tf_op jit(solution)/shard_map/ppermute | solution.py:21
  135.7 24.3 %collective-permute-start.12 = (bf16[4,64,2048]{2,1,0:T(8,128)(2,1)}, bf16[4,64,2048]{2,1,0:T(8,128)(2,1)}, u32[]{:S(2)}, u32[]{:S(2)}) collective-permute-start(bf16[4,64,2048]{2,1,0:T(8,128)(2,1)} %shard_map.77), channel_id=1, source_target_pairs={{0,1},{1,0},{2,3},{3,2},{4,5},{5,4},{6,7},{7,6},{8,9},{9,8},{10,11... | collective-permute-start | bytes 3145736 | tf_op jit(solution)/shard_map/ppermute | solution.py:21
  147.9 29.5 %all-to-all-start.3 = ((bf16[32,72,128]{2,1,0:T(8,128)(2,1)}), bf16[32,72,128]{2,1,0:T(8,128)(2,1)S(1)}, u32[]{:S(2)}, u32[]{:S(2)}) async-start(bf16[32,72,128]{2,1,0:T(8,128)(2,1)} %bitcast.58), calls=%async_computation.3 | async-start | bytes 1179648 | tf_op jit(solution)/shard_map/all_to_all | solution.py:25
  168.6 13.6 %collective-permute-start.13 = (bf16[8,2,32,256]{3,2,1,0:T(8,128)(2,1)}, bf16[8,2,32,256]{3,2,1,0:T(8,128)(2,1)S(1)}, u32[]{:S(2)}, u32[]{:S(2)}) collective-permute-start(bf16[8,2,32,256]{3,2,1,0:T(8,128)(2,1)} %get-tuple-element.5), channel_id=1, source_target_pairs={{0,1},{1,0},{2,3},{3,2},{4,5},{5,4},{6,7},{7,6},{8,9},{9,8},{10,11... | collective-permute-start | bytes 786440 | tf_op jit(solution)/shard_map/ppermute | solution.py:21
  177.5 8.3 %collective-permute-start.16 = (f32[8,128]{1,0:T(8,128)S(1)}, f32[8,128]{1,0:T(8,128)S(1)}, u32[]{:S(2)}, u32[]{:S(2)}) collective-permute-start(f32[8,128]{1,0:T(8,128)S(1)} %slice_reduce_fusion.1), channel_id=1, source_target_pairs={{0,4},{4,0},{1,5},{5,1},{2,6},{6,2},{3,7},{7,3},{8,12},{12,8},{9,1... | collective-permute-start | bytes 12296 | tf_op jit(solution)/shard_map/ppermute | solution.py:21
  (7 other events, 52.3 us)

commit v2 on v1

v2 whole, which is shorter than its diff:
```python
import jax
import jax.numpy as jnp
from jax import lax
from jax.experimental import pallas as pl
from jax.experimental.pallas import tpu as pltpu
from jax.sharding import Mesh
from jax.sharding import PartitionSpec as P

STATE = ("state_0", "state_1")
ROW = "bond_0"
FAR = "bond_1"
NEAR = "bond_2"
CORE = "bond_3"


ORDER = (0, 7, 1, 6, 2, 5, 3, 4)


def shifted(value, axis, step):
    size = lax.axis_size(axis)
    return lax.ppermute(value, axis, [(i, (i + step) % size) for i in range(size)])


def exchanged(value, axis):
    return lax.all_to_all(value, axis, split_axis=0, concat_axis=0, tiled=True)


def sent_to_all(value, axis):
    return exchanged(jnp.broadcast_to(value, (lax.axis_size(axis), *value.shape)), axis)


def rows_times(left, right):
    return lax.dot_general(left, right, (((1,), (1,)), ((), ())), preferred_element_type=jnp.float32)


def paired(pieces):
    for step in range(0, len(ORDER), 2):
        last = len(pieces) if step + 2 == len(ORDER) else step + 2
        left = jnp.concatenate([piece[...] for piece in pieces[step:last]])
        yield left, ORDER[step : step + 2]


def join_kernel(*refs):
    *pieces, out = refs
    for k, piece in enumerate(pieces):
        out[k] = piece[...]


def joined(*pieces):
    resident = pl.BlockSpec(memory_space=pltpu.VMEM)
    return pl.pallas_call(
        join_kernel,
        out_shape=jax.ShapeDtypeStruct((len(pieces), *pieces[0].shape), pieces[0].dtype),
        in_specs=[resident] * len(pieces),
        out_specs=resident,
    )(*pieces)


def project_kernel(*refs):
    pieces = refs[:9]
    mine, other, seen, out = refs[9:]
    z = lax.axis_index(ROW)
    c = lax.axis_index(CORE)
    height, count = seen.shape[2:]
    rows, cores = out.shape[:2]
    right = jnp.concatenate([mine[...], other[...]])
    total = jnp.zeros((height, count), jnp.float32)
    for left, offsets in paired(pieces):
        product = rows_times(left, right)
        for i, offset in enumerate(offsets):
            place = lax.rem(z + offset, rows)
            for k in range(cores):
                target = lax.rem(c + k, cores)
                one = product[i * height : (i + 1) * height, k * count : (k + 1) * count]
                out[place, target, :height] = one.astype(jnp.bfloat16)
                current = seen[place, target]
                total += one * current.astype(jnp.float32)
    whole = jnp.full((8, count), jnp.sum(total), jnp.float32)
    high = whole.astype(jnp.bfloat16).astype(jnp.float32)
    middle = (whole - high).astype(jnp.bfloat16).astype(jnp.float32)
    low = whole - high - middle
    row = lax.broadcasted_iota(jnp.int32, whole.shape, 0)
    parts = jnp.where(row == 0, high, jnp.where(row == 1, middle, jnp.where(row == 2, low, 0.0)))
    for i in range(rows):
        for k in range(cores):
            out[i, k, height:] = parts.astype(jnp.bfloat16)


def grow_kernel(*refs):
    pieces = refs[:9]
    stored = refs[9:13]
    spread, keep, give, operand, moved, semaphores = refs[13:]
    z = lax.axis_index(ROW)
    u = lax.axis_index(FAR)
    v = lax.axis_index(NEAR)
    c = lax.axis_index(CORE)
    copies = []
    for k, source in enumerate(stored):
        for near in range(2):
            column = lax.rem(u + k % 2, 2) * 2 + lax.rem(v + k % 2 + near, 2)
            slot = column * 2 + lax.rem(c + k // 2, 2)
            for s in range(operand.shape[0]):
                copy = pltpu.make_async_copy(
                    source.at[near, s], operand.at[s, slot], semaphores.at[len(copies)]
                )
                copy.start()
                copies.append(copy)
    for copy in copies:
        copy.wait()
    physical, slots, width, bond = operand.shape
    block = slots * width
    rows, height, _ = moved.shape
    wide = spread.shape[0]
    lanes = spread.shape[4]
    part = lanes // physical
    right = operand[...].reshape(physical * block, bond)
    for left, offsets in paired(pieces):
        product = rows_times(left, right).astype(jnp.bfloat16)
        for i, offset in enumerate(offsets):
            moved[lax.rem(z + offset, rows)] = product[i * height : (i + 1) * height]
    inner = moved[...].reshape(rows * height, physical * block)
    for k in range(keep.shape[0]):
        left = spread[k % wide, k // wide].reshape(rows * height, lanes)
        crossed = lax.dot_general(
            left, inner, (((0,), (0,)), ((), ())), preferred_element_type=jnp.float32
        )
        total = crossed[:part, :block]
        for s in range(1, physical):
            total += crossed[s * part : (s + 1) * part, s * block : (s + 1) * block]
        first, second = total[:width], total[width:]
        keep[k] = jnp.where(c == 0, first, second)
        give[k] = jnp.where(c == 0, second, first).astype(jnp.bfloat16)


def whole(intersect_left, stored_block, stored_site, current_site, current_block, penalty_weight):
    states = lax.axis_size(STATE)
    rows = lax.axis_size(ROW)
    pairs, width, bond = stored_block.shape[1:]
    physical = stored_site.shape[1]
    block = current_block.shape[2]
    columns = 4
    count = pairs * width
    height = columns * width
    part = block // columns
    column = (FAR, NEAR)
    group = (*STATE, CORE)
    anywhere = pl.BlockSpec(memory_space=pl.ANY)
    resident = pl.BlockSpec(memory_space=pltpu.VMEM)

    mine = intersect_left[0]
    other = shifted(mine, NEAR, 1)
    first = lax.axis_index(NEAR) == 0
    mine = jnp.where(first, jnp.stack([mine, other]), jnp.stack([other, mine]))
    other = lax.ppermute(mine, column, [(i, 3 - i) for i in range(4)])
    first = lax.axis_index(FAR) == 0
    environment = jnp.where(first, jnp.stack([mine, other]), jnp.stack([other, mine]))
    environment = environment.reshape(height, bond)

    site = current_site.reshape(width, physical, columns, part).transpose(2, 0, 1, 3)
    site = exchanged(site.reshape(columns, width, physical * part), column)
    site = site.reshape(height, physical * part)

    site = sent_to_all(site, (STATE[0], ROW))
    spread = sent_to_all(site, STATE[1]).reshape(-1, 2, rows, height, physical * part)

    turned = current_block.reshape(count, block).T.reshape(columns, 2, width, count)
    turned = turned.transpose(1, 0, 2, 3).reshape(2, height, count)
    turned = jnp.broadcast_to(turned, (states, *turned.shape)).reshape(-1, height, count)
    seen = exchanged(turned, group).reshape(states, 2, height, count)

    pieces = [environment]
    below = above = environment
    for _ in range(1, rows // 2):
        below = shifted(below, ROW, 1)
        above = shifted(above, ROW, -1)
        pieces += [below, above]
    pieces.append(shifted(below[: height // 2], ROW, 1))
    pieces.append(shifted(above[height // 2 :], ROW, -1))

    local = stored_site[0].reshape(physical * width, bond)
    site_near = shifted(local, NEAR, 1)
    site_pair = joined(local, site_near).reshape(2, physical, width, bond)
    site_far = lax.ppermute(site_pair, (FAR, NEAR), [(i, 3 - i) for i in range(4)])
    site_pair_other = shifted(site_pair, CORE, 1)
    site_far_other = shifted(site_far, CORE, 1)

    stored = stored_block[0].reshape(count, bond)
    stored_other = shifted(stored, CORE, 1)

    projected = pl.pallas_call(
        project_kernel,
        out_shape=jax.ShapeDtypeStruct((rows, 2, height + 8, count), jnp.bfloat16),
        in_specs=[resident] * 12,
        out_specs=resident,
        cost_estimate=pl.CostEstimate(flops=2 * 512 * 512 * 2048, bytes_accessed=5 << 20, transcendentals=0),
        name="project",
    )(*pieces, stored, stored_other, seen)

    received = exchanged(projected.reshape(-1, height + 8, count), group)
    received = received.reshape(states, 2, height + 8, count).astype(jnp.float32)
    total = received[:, :, height : height + 3].sum(axis=(1, 2))
    total = sent_to_all(total, column).sum(axis=0)

    keep, give = pl.pallas_call(
        grow_kernel,
        out_shape=(
            jax.ShapeDtypeStruct((states, width, block), jnp.float32),
            jax.ShapeDtypeStruct((states, width, block), jnp.bfloat16),
        ),
        in_specs=[resident] * 9 + [anywhere] * 4 + [resident],
        out_specs=(resident, resident),
        scratch_shapes=[
            pltpu.VMEM((physical, 8, width, bond), jnp.bfloat16),
            pltpu.VMEM((rows, height, physical * block), jnp.bfloat16),
            pltpu.SemaphoreType.DMA((16,)),
        ],
        cost_estimate=pl.CostEstimate(flops=3 * 512 * 512 * 2048, bytes_accessed=6 << 20, transcendentals=0),
        name="grow",
    )(*pieces, site_pair, site_far, site_pair_other, site_far_other, spread)
    got = shifted(give, CORE, 1)
    grown = (keep + got.astype(jnp.float32)).astype(jnp.bfloat16)

    total = jnp.broadcast_to(total[:, :1], (states, block))
    high = lax.reduce_precision(total, 8, 7)
    middle = lax.reduce_precision(total - high, 8, 7)
    low = total - high - middle
    lane = lax.broadcasted_iota(jnp.int32, total.shape, 1)
    parts = jnp.where(lane == 0, high, jnp.where(lane == 1, middle, jnp.where(lane == 2, low, 0.0)))
    parts = jnp.broadcast_to(parts.astype(jnp.bfloat16), (states, states, block))
    grown = jnp.concatenate([grown, parts], axis=1)
    grown = exchanged(grown, ROW)
    intersect = grown[:, width:, :3].astype(jnp.float32).sum(axis=(0, 2))
    intersect = intersect * (1.0 / (physical * bond))
    intersect_next = grown[:, :width].transpose(1, 0, 2).reshape(1, width, rows * block)

    gain = penalty_weight * intersect
    summed = jnp.sum(gain[:, None, None, None] * received[:, :, :height], axis=0)
    summed = summed.reshape(2, columns, width, count).transpose(1, 0, 2, 3).reshape(block, count)
    penalized = current_block.astype(jnp.float32) + summed.T.reshape(pairs, width, block)
    return (penalized, intersect_next)


def solution(mesh):
    torus = Mesh(
        mesh.devices.reshape(2, mesh.shape["state"] // 2, 8, 2, 2, 2),
        (*STATE, ROW, FAR, NEAR, CORE),
    )
    bond = (ROW, FAR, NEAR, CORE)
    in_specs = (
        P(STATE, bond, None),
        P(STATE, None, bond, None),
        P(STATE, None, bond, None),
        P(bond, None, STATE),
        P(None, bond, STATE),
        P(),
    )
    out_specs = (P(None, bond, STATE), P(STATE, bond, None))
    return jax.shard_map(whole, mesh=torus, in_specs=in_specs, out_specs=out_specs, check_vma=False)
```

time: 206 us -> 199 us (0.966)
  the two profiles are of different devices: /device:TPU:1 before, /device:TPU:10 now
where the time goes in v2:
time: 199 us; the launch traced here: 198 us
  starting transfers between devices  84.9 us (43%)
  waiting for transfers between devices  66.8 us (34%)
  blocking collectives  15.8 us (8%)
  Pallas kernels  15.7 us (8%)
  local copies, waits for them, and re-layouts  12 us (6%)
    ppermute x14, starting transfers between devices, shifted(): lax.ppermute(value, axis, [(i, (i + step) % size) for i in range(size)])  40.6 us
    all_to_all x6, starting transfers between devices, exchanged(): return lax.all_to_all(value, axis, split_axis=0, concat_axis=0, tiled=True)  38.4 us
    all_to_all x6, waiting for transfers between devices, exchanged(): return lax.all_to_all(value, axis, split_axis=0, concat_axis=0, tiled=True)  21.4 us
    ppermute x14, waiting for transfers between devices, shifted(): lax.ppermute(value, axis, [(i, (i + step) % size) for i in range(size)])  17 us
    ppermute x1, waiting for transfers between devices, whole(): other = lax.ppermute(mine, column, [(i, 3 - i) for i in range(4)])  15.9 us
    all_to_all x1, blocking collectives, exchanged(): return lax.all_to_all(value, axis, split_axis=0, concat_axis=0, tiled=True)  15.8 us
    ppermute x1, waiting for transfers between devices, whole(): lax.ppermute(site_pair, (FAR, NEAR), [(i, 3 - i) for i in range(4)])  12.5 us
    pallas_call x1, Pallas kernels, whole(): pl.pallas_call(grow_kernel, out_shape=(jax.ShapeDtypeStruct((states, widt...  9 us
  transfers between devices with their start and end apart: 22, of which 9 were waited for; matrix products, arithmetic and copies ran while one was open for 3% of the time, Pallas kernels for 8%

profile of v2, /device:TPU:10, one launch (start us, length us, event | category | flops | bytes accessed | tf_op | source)
XLA Modules:
  0.0 197.7 jit_solution(6530078581548215423)
XLA Ops:
  2.3 6.2 %all-to-all-start = ((bf16[4,32,128]{2,1,0:T(8,128)(2,1)}), bf16[4,32,128]{2,1,0:T(8,128)(2,1)S(1)}, u32[]{:S(2)}, u32[]{:S(2)}) async-start(bf16[4,32,128]{2,1,0:T(8,128)(2,1)} %reshape.117), calls=%async_computation | async-start | bytes 65536 | tf_op jit(solution)/shard_map/all_to_all | solution.py:25
  9.5 6.9 %all-to-all-done = bf16[4,32,128]{2,1,0:T(8,128)(2,1)S(1)} async-done(((bf16[4,32,128]{2,1,0:T(8,128)(2,1)}), bf16[4,32,128]{2,1,0:T(8,128)(2,1)S(1)}, u32[]{:S(2)}, u32[]{:S(2)}) %all-to-all-start) | async-done | bytes 32800 | tf_op jit(solution)/shard_map/all_to_all | solution.py:25
  17.3 6.2 %all-to-all-start.3 = ((bf16[16,128,128]{2,1,0:T(8,128)(2,1)}), bf16[16,128,128]{2,1,0:T(8,128)(2,1)S(1)}, u32[]{:S(2)}, u32[]{:S(2)}) async-start(bf16[16,128,128]{2,1,0:T(8,128)(2,1)} %bitcast.17), calls=%async_computation.3 | async-start | bytes 1048576 | tf_op jit(solution)/shard_map/all_to_all | solution.py:25
  23.5 2.5 %collective-permute-start = (bf16[32,2048]{1,0:T(8,128)(2,1)S(1)}, bf16[32,2048]{1,0:T(8,128)(2,1)S(1)}, u32[]{:S(2)}, u32[]{:S(2)}) collective-permute-start(bf16[32,2048]{1,0:T(8,128)(2,1)S(1)} %bitcast.48), channel_id=1, source_target_pairs={{0,2},{2,0},{1,3},{3,1},{4,6},{6,4},{5,7},{7,5},{8,10},{10,8},{9,1... | collective-permute-start | bytes 393224 | tf_op jit(solution)/shard_map/ppermute | solution.py:21
  26.0 6.8 %all-to-all-done.3 = bf16[16,128,128]{2,1,0:T(8,128)(2,1)S(1)} async-done(((bf16[16,128,128]{2,1,0:T(8,128)(2,1)}), bf16[16,128,128]{2,1,0:T(8,128)(2,1)S(1)}, u32[]{:S(2)}, u32[]{:S(2)}) %all-to-all-start.3) | async-done | bytes 524320 | tf_op jit(solution)/shard_map/all_to_all | solution.py:25
  33.7 11.3 %all-to-all-start.1 = ((bf16[16,128,128]{2,1,0:T(8,128)(2,1)}), bf16[16,128,128]{2,1,0:T(8,128)(2,1)S(1)}, u32[]{:S(2)}, u32[]{:S(2)}) async-start(bf16[16,128,128]{2,1,0:T(8,128)(2,1)} %broadcast_in_dim.31), calls=%async_computation.1 | async-start | bytes 1048576 | tf_op jit(solution)/shard_map/all_to_all | solution.py:25
  47.1 15.9 %collective-permute-done.1 = bf16[2,32,2048]{2,1,0:T(8,128)(2,1)S(1)} collective-permute-done((bf16[2,32,2048]{2,1,0:T(8,128)(2,1)S(1)}, bf16[2,32,2048]{2,1,0:T(8,128)(2,1)S(1)}, u32[]{:S(2)}, u32[]{:S(2)}) %collective-permute-start.1) | collective-permute-done | bytes 262176 | tf_op jit(solution)/shard_map/ppermute | solution.py:154
  63.1 3.6 %collective-permute-start.2 = (bf16[128,2048]{1,0:T(8,128)(2,1)S(1)}, bf16[128,2048]{1,0:T(8,128)(2,1)S(1)}, u32[]{:S(2)}, u32[]{:S(2)}) collective-permute-start(bf16[128,2048]{1,0:T(8,128)(2,1)S(1)} %bitcast.37), channel_id=1, source_target_pairs={{0,8},{8,16},{16,24},{24,32},{32,40},{40,48},{48,56},{56,0},{1,9},... | collective-permute-start | bytes 1572872 | tf_op jit(solution)/shard_map/ppermute | solution.py:21
  66.6 3.5 %collective-permute-start.3 = (bf16[128,2048]{1,0:T(8,128)(2,1)S(1)}, bf16[128,2048]{1,0:T(8,128)(2,1)}, u32[]{:S(2)}, u32[]{:S(2)}) collective-permute-start(bf16[128,2048]{1,0:T(8,128)(2,1)S(1)} %bitcast.38), channel_id=1, source_target_pairs={{0,56},{8,0},{16,8},{24,16},{32,24},{40,32},{48,40},{56,48},{1,57}... | collective-permute-start | bytes 1572872 | tf_op jit(solution)/shard_map/ppermute | solution.py:21
  72.0 5.6 %all-to-all-start.2 = ((bf16[4,16,128,128]{3,2,1,0:T(8,128)(2,1)}), bf16[4,16,128,128]{3,2,1,0:T(8,128)(2,1)S(1)}, u32[]{:S(2)}, u32[]{:S(2)}) async-start(bf16[4,16,128,128]{3,2,1,0:T(8,128)(2,1)} %broadcast_in_dim.32), calls=%async_computation.2 | async-start | bytes 4194304 | tf_op jit(solution)/shard_map/all_to_all | solution.py:25
  77.6 2.4 %collective-permute-done.2.refs_1_ = bf16[128,2048]{1,0:T(8,128)(2,1)S(1)} collective-permute-done((bf16[128,2048]{1,0:T(8,128)(2,1)S(1)}, bf16[128,2048]{1,0:T(8,128)(2,1)S(1)}, u32[]{:S(2)}, u32[]{:S(2)}) %collective-permute-start.2) | collective-permute-done | bytes 524320 | tf_op jit(solution)/shard_map/ppermute | solution.py:21
  82.4 4.7 %collective-permute-start.5 = (bf16[128,2048]{1,0:T(8,128)(2,1)}, bf16[128,2048]{1,0:T(8,128)(2,1)S(1)}, u32[]{:S(2)}, u32[]{:S(2)}) collective-permute-start(bf16[128,2048]{1,0:T(8,128)(2,1)} %collective-permute-done.3.refs_2_), channel_id=1, source_target_pairs={{0,56},{8,0},{16,8},{24,16},{32,24},{40,32},{48,40},{56,48},{1,57}... | collective-permute-start | bytes 1572872 | tf_op jit(solution)/shard_map/ppermute | solution.py:21
  87.1 9.0 %collective-permute-done.4.refs_3_ = bf16[128,2048]{1,0:T(8,128)(2,1)S(1)} collective-permute-done((bf16[128,2048]{1,0:T(8,128)(2,1)S(1)}, bf16[128,2048]{1,0:T(8,128)(2,1)S(1)}, u32[]{:S(2)}, u32[]{:S(2)}) %collective-permute-start.4) | collective-permute-done | bytes 524320 | tf_op jit(solution)/shard_map/ppermute | solution.py:21
  98.1 5.1 %collective-permute-start.7 = (bf16[128,2048]{1,0:T(8,128)(2,1)S(1)}, bf16[128,2048]{1,0:T(8,128)(2,1)S(1)}, u32[]{:S(2)}, u32[]{:S(2)}) collective-permute-start(bf16[128,2048]{1,0:T(8,128)(2,1)S(1)} %collective-permute-done.5.refs_4_), channel_id=1, source_target_pairs={{0,56},{8,0},{16,8},{24,16},{32,24},{40,32},{48,40},{56,48},{1,57}... | collective-permute-start | bytes 1572872 | tf_op jit(solution)/shard_map/ppermute | solution.py:21
  107.1 4.3 %collective-permute-done.6.refs_5_ = bf16[128,2048]{1,0:T(8,128)(2,1)S(1)} collective-permute-done((bf16[128,2048]{1,0:T(8,128)(2,1)S(1)}, bf16[128,2048]{1,0:T(8,128)(2,1)S(1)}, u32[]{:S(2)}, u32[]{:S(2)}) %collective-permute-start.6) | collective-permute-done | bytes 524320 | tf_op jit(solution)/shard_map/ppermute | solution.py:21
  114.9 5.1 %collective-permute-start.9 = (bf16[64,2048]{1,0:T(8,128)(2,1)}, bf16[64,2048]{1,0:T(8,128)(2,1)}, u32[]{:S(2)}, u32[]{:S(2)}) collective-permute-start(bf16[64,2048]{1,0:T(8,128)(2,1)} %slice.29), channel_id=1, source_target_pairs={{0,56},{8,0},{16,8},{24,16},{32,24},{40,32},{48,40},{56,48},{1,57}... | collective-permute-start | bytes 786440 | tf_op jit(solution)/shard_map/ppermute | solution.py:21
  121.9 4.0 %collective-permute-start.11 = (bf16[2,2,32,2048]{3,2,1,0:T(8,128)(2,1)}, bf16[2,2,32,2048]{3,2,1,0:T(8,128)(2,1)}, u32[]{:S(2)}, u32[]{:S(2)}) collective-permute-start(bf16[2,2,32,2048]{3,2,1,0:T(8,128)(2,1)} %bitcast.43), channel_id=1, source_target_pairs={{0,6},{2,4},{4,2},{6,0},{1,7},{3,5},{5,3},{7,1},{8,14},{10,12},{12... | collective-permute-start | bytes 1572872 | tf_op jit(solution)/shard_map/ppermute | solution.py:183
  126.7 4.9 %project.1 = bf16[8,2,136,128]{3,2,1,0:T(8,128)(2,1)} custom-call(bf16[128,2048]{1,0:T(8,128)(2,1)} %bitcast.39, bf16[128,2048]{1,0:T(8,128)(2,1)} %copy-done.4, bf16[128,2048]{1,0:T(8,128)(2,1)} %collective-permute-done.3.refs_2_, bf16[128,2048]{1,0:T(8,128)(2,1)} %copy-done.5, bf16[128,2048]{1,0:T(8,128)(2,1)} %copy-done.6, bf16[128,2048]{1,0:T(8,128)(2,1)} %copy-done.2, ...), custom_call_target="tpu_custom_call" | custom-call | flops 1073741824 | bytes 5242880 | tf_op jit(solution)/shard_map/project/pallas_call | solution.py:190
  131.6 4.7 %all-to-all-start.4 = ((bf16[16,136,128]{2,1,0:T(8,128)(2,1)}), bf16[16,136,128]{2,1,0:T(8,128)(2,1)S(1)}, u32[]{:S(2)}, u32[]{:S(2)}) async-start(bf16[16,136,128]{2,1,0:T(8,128)(2,1)} %bitcast.41), calls=%async_computation.4 | async-start | bytes 1114112 | tf_op jit(solution)/shard_map/all_to_all | solution.py:25
  138.3 12.5 %collective-permute-done.11.refs_10_ = bf16[2,2,32,2048]{3,2,1,0:T(8,128)(2,1)} collective-permute-done((bf16[2,2,32,2048]{3,2,1,0:T(8,128)(2,1)}, bf16[2,2,32,2048]{3,2,1,0:T(8,128)(2,1)}, u32[]{:S(2)}, u32[]{:S(2)}) %collective-permute-start.11) | collective-permute-done | bytes 524320 | tf_op jit(solution)/shard_map/ppermute | solution.py:183
  155.6 9.0 %grow.1 = (f32[8,32,256]{2,1,0:T(8,128)}, bf16[8,32,256]{2,1,0:T(8,128)(2,1)}) custom-call(bf16[128,2048]{1,0:T(8,128)(2,1)} %bitcast.40, bf16[128,2048]{1,0:T(8,128)(2,1)} %copy-done.4, bf16[128,2048]{1,0:T(8,128)(2,1)} %collective-permute-done.3.refs_2_, bf16[128,2048]{1,0:T(8,128)(2,1)} %copy-done.5, bf16[128,2048]{1,0:T(8,128)(2,1)} %copy-done.6, ...), custom_call_target="tpu_custom_call" | custom-call | flops 1610612736 | bytes 6291456 | tf_op jit(solution)/shard_map/grow/pallas_call | solution.py:204
  167.6 4.4 %all-to-all-start.5 = ((f32[4,8,128]{2,1,0:T(8,128)}), f32[4,8,128]{2,1,0:T(8,128)S(1)}, u32[]{:S(2)}, u32[]{:S(2)}) async-start(f32[4,8,128]{2,1,0:T(8,128)} %broadcast_in_dim.34), calls=%async_computation.5 | async-start | bytes 32768 | tf_op jit(solution)/shard_map/all_to_all | solution.py:25
  172.0 7.7 %all-to-all-done.5 = f32[4,8,128]{2,1,0:T(8,128)S(1)} async-done(((f32[4,8,128]{2,1,0:T(8,128)}), f32[4,8,128]{2,1,0:T(8,128)S(1)}, u32[]{:S(2)}, u32[]{:S(2)}) %all-to-all-start.5) | async-done | bytes 16416 | tf_op jit(solution)/shard_map/all_to_all | solution.py:25
  180.0 15.8 %all_to_all.35 = bf16[8,40,256]{2,1,0:T(8,128)(2,1)S(1)} all-to-all(bf16[8,40,256]{2,1,0:T(8,128)(2,1)S(1)} %pad_maximum_fusion), channel_id=1, replica_groups=mesh['state_0'=2,'state_1'=4,'bond_0'=8,'bond_1'=2,'bond_2'=2,'bond_3'=2..., dimensions={0} | all-to-all | bytes 327680 | tf_op jit(solution)/shard_map/all_to_all | solution.py:25
  (90 shorter events, 34.4 us)
Async XLA Ops:
  2.3 14.1 %all-to-all-start = ((bf16[4,32,128]{2,1,0:T(8,128)(2,1)}), bf16[4,32,128]{2,1,0:T(8,128)(2,1)S(1)}, u32[]{:S(2)}, u32[]{:S(2)}) async-start(bf16[4,32,128]{2,1,0:T(8,128)(2,1)} %reshape.117), calls=%async_computation | async-start | bytes 65536 | tf_op jit(solution)/shard_map/all_to_all | solution.py:25
  17.3 15.5 %all-to-all-start.3 = ((bf16[16,128,128]{2,1,0:T(8,128)(2,1)}), bf16[16,128,128]{2,1,0:T(8,128)(2,1)S(1)}, u32[]{:S(2)}, u32[]{:S(2)}) async-start(bf16[16,128,128]{2,1,0:T(8,128)(2,1)} %bitcast.17), calls=%async_computation.3 | async-start | bytes 1048576 | tf_op jit(solution)/shard_map/all_to_all | solution.py:25
  23.5 21.5 %collective-permute-start = (bf16[32,2048]{1,0:T(8,128)(2,1)S(1)}, bf16[32,2048]{1,0:T(8,128)(2,1)S(1)}, u32[]{:S(2)}, u32[]{:S(2)}) collective-permute-start(bf16[32,2048]{1,0:T(8,128)(2,1)S(1)} %bitcast.48), channel_id=1, source_target_pairs={{0,2},{2,0},{1,3},{3,1},{4,6},{6,4},{5,7},{7,5},{8,10},{10,8},{9,1... | collective-permute-start | bytes 393224 | tf_op jit(solution)/shard_map/ppermute | solution.py:21
  33.7 36.4 %all-to-all-start.1 = ((bf16[16,128,128]{2,1,0:T(8,128)(2,1)}), bf16[16,128,128]{2,1,0:T(8,128)(2,1)S(1)}, u32[]{:S(2)}, u32[]{:S(2)}) async-start(bf16[16,128,128]{2,1,0:T(8,128)(2,1)} %broadcast_in_dim.31), calls=%async_computation.1 | async-start | bytes 1048576 | tf_op jit(solution)/shard_map/all_to_all | solution.py:25
  45.1 17.9 %collective-permute-start.1 = (bf16[2,32,2048]{2,1,0:T(8,128)(2,1)S(1)}, bf16[2,32,2048]{2,1,0:T(8,128)(2,1)S(1)}, u32[]{:S(2)}, u32[]{:S(2)}) collective-permute-start(bf16[2,32,2048]{2,1,0:T(8,128)(2,1)S(1)} %maximum_select_fusion.2), channel_id=1, source_target_pairs={{0,6},{2,4},{4,2},{6,0},{1,7},{3,5},{5,3},{7,1},{8,14},{10,12},{12... | collective-permute-start | bytes 786440 | tf_op jit(solution)/shard_map/ppermute | solution.py:154
  63.1 17.0 %collective-permute-start.2 = (bf16[128,2048]{1,0:T(8,128)(2,1)S(1)}, bf16[128,2048]{1,0:T(8,128)(2,1)S(1)}, u32[]{:S(2)}, u32[]{:S(2)}) collective-permute-start(bf16[128,2048]{1,0:T(8,128)(2,1)S(1)} %bitcast.37), channel_id=1, source_target_pairs={{0,8},{8,16},{16,24},{24,32},{32,40},{40,48},{48,56},{56,0},{1,9},... | collective-permute-start | bytes 1572872 | tf_op jit(solution)/shard_map/ppermute | solution.py:21
  66.6 15.7 %collective-permute-start.3 = (bf16[128,2048]{1,0:T(8,128)(2,1)S(1)}, bf16[128,2048]{1,0:T(8,128)(2,1)}, u32[]{:S(2)}, u32[]{:S(2)}) collective-permute-start(bf16[128,2048]{1,0:T(8,128)(2,1)S(1)} %bitcast.38), channel_id=1, source_target_pairs={{0,56},{8,0},{16,8},{24,16},{32,24},{40,32},{48,40},{56,48},{1,57}... | collective-permute-start | bytes 1572872 | tf_op jit(solution)/shard_map/ppermute | solution.py:21
  72.0 59.5 %all-to-all-start.2 = ((bf16[4,16,128,128]{3,2,1,0:T(8,128)(2,1)}), bf16[4,16,128,128]{3,2,1,0:T(8,128)(2,1)S(1)}, u32[]{:S(2)}, u32[]{:S(2)}) async-start(bf16[4,16,128,128]{3,2,1,0:T(8,128)(2,1)} %broadcast_in_dim.32), calls=%async_computation.2 | async-start | bytes 4194304 | tf_op jit(solution)/shard_map/all_to_all | solution.py:25
  80.0 16.1 %collective-permute-start.4 = (bf16[128,2048]{1,0:T(8,128)(2,1)S(1)}, bf16[128,2048]{1,0:T(8,128)(2,1)S(1)}, u32[]{:S(2)}, u32[]{:S(2)}) collective-permute-start(bf16[128,2048]{1,0:T(8,128)(2,1)S(1)} %collective-permute-done.2.refs_1_), channel_id=1, source_target_pairs={{0,8},{8,16},{16,24},{24,32},{32,40},{40,48},{48,56},{56,0},{1,9},... | collective-permute-start | bytes 1572872 | tf_op jit(solution)/shard_map/ppermute | solution.py:21
  82.4 15.7 %collective-permute-start.5 = (bf16[128,2048]{1,0:T(8,128)(2,1)}, bf16[128,2048]{1,0:T(8,128)(2,1)S(1)}, u32[]{:S(2)}, u32[]{:S(2)}) collective-permute-start(bf16[128,2048]{1,0:T(8,128)(2,1)} %collective-permute-done.3.refs_2_), channel_id=1, source_target_pairs={{0,56},{8,0},{16,8},{24,16},{32,24},{40,32},{48,40},{56,48},{1,57}... | collective-permute-start | bytes 1572872 | tf_op jit(solution)/shard_map/ppermute | solution.py:21
  96.2 15.3 %collective-permute-start.6 = (bf16[128,2048]{1,0:T(8,128)(2,1)S(1)}, bf16[128,2048]{1,0:T(8,128)(2,1)S(1)}, u32[]{:S(2)}, u32[]{:S(2)}) collective-permute-start(bf16[128,2048]{1,0:T(8,128)(2,1)S(1)} %collective-permute-done.4.refs_3_), channel_id=1, source_target_pairs={{0,8},{8,16},{16,24},{24,32},{32,40},{40,48},{48,56},{56,0},{1,9},... | collective-permute-start | bytes 1572872 | tf_op jit(solution)/shard_map/ppermute | solution.py:21
  98.1 16.0 %collective-permute-start.7 = (bf16[128,2048]{1,0:T(8,128)(2,1)S(1)}, bf16[128,2048]{1,0:T(8,128)(2,1)S(1)}, u32[]{:S(2)}, u32[]{:S(2)}) collective-permute-start(bf16[128,2048]{1,0:T(8,128)(2,1)S(1)} %collective-permute-done.5.refs_4_), channel_id=1, source_target_pairs={{0,56},{8,0},{16,8},{24,16},{32,24},{40,32},{48,40},{56,48},{1,57}... | collective-permute-start | bytes 1572872 | tf_op jit(solution)/shard_map/ppermute | solution.py:21
  103.2 22.7 %collective-permute-start.15 = (bf16[128,2048]{1,0:T(8,128)(2,1)}, bf16[128,2048]{1,0:T(8,128)(2,1)}, u32[]{:S(2)}, u32[]{:S(2)}) collective-permute-start(bf16[128,2048]{1,0:T(8,128)(2,1)} %bitcast.46), channel_id=1, source_target_pairs={{0,1},{1,0},{2,3},{3,2},{4,5},{5,4},{6,7},{7,6},{8,9},{9,8},{10,11... | collective-permute-start | bytes 1572872 | tf_op jit(solution)/shard_map/ppermute | solution.py:21
  105.2 14.9 %collective-permute-start.10 = (bf16[64,2048]{1,0:T(8,128)(2,1)}, bf16[64,2048]{1,0:T(8,128)(2,1)}, u32[]{:S(2)}, u32[]{:S(2)}) collective-permute-start(bf16[64,2048]{1,0:T(8,128)(2,1)} %bitcast.6.refs_0_), channel_id=1, source_target_pairs={{0,2},{2,0},{1,3},{3,1},{4,6},{6,4},{5,7},{7,5},{8,10},{10,8},{9,1... | collective-permute-start | bytes 786440 | tf_op jit(solution)/shard_map/ppermute | solution.py:21
  112.2 13.7 %collective-permute-start.8 = (bf16[64,2048]{1,0:T(8,128)(2,1)}, bf16[64,2048]{1,0:T(8,128)(2,1)S(1)}, u32[]{:S(2)}, u32[]{:S(2)}) collective-permute-start(bf16[64,2048]{1,0:T(8,128)(2,1)} %slice.28), channel_id=1, source_target_pairs={{0,8},{8,16},{16,24},{24,32},{32,40},{40,48},{48,56},{56,0},{1,9},... | collective-permute-start | bytes 786440 | tf_op jit(solution)/shard_map/ppermute | solution.py:21
  114.9 11.0 %collective-permute-start.9 = (bf16[64,2048]{1,0:T(8,128)(2,1)}, bf16[64,2048]{1,0:T(8,128)(2,1)}, u32[]{:S(2)}, u32[]{:S(2)}) collective-permute-start(bf16[64,2048]{1,0:T(8,128)(2,1)} %slice.29), channel_id=1, source_target_pairs={{0,56},{8,0},{16,8},{24,16},{32,24},{40,32},{48,40},{56,48},{1,57}... | collective-permute-start | bytes 786440 | tf_op jit(solution)/shard_map/ppermute | solution.py:21
  121.9 28.8 %collective-permute-start.11 = (bf16[2,2,32,2048]{3,2,1,0:T(8,128)(2,1)}, bf16[2,2,32,2048]{3,2,1,0:T(8,128)(2,1)}, u32[]{:S(2)}, u32[]{:S(2)}) collective-permute-start(bf16[2,2,32,2048]{3,2,1,0:T(8,128)(2,1)} %bitcast.43), channel_id=1, source_target_pairs={{0,6},{2,4},{4,2},{6,0},{1,7},{3,5},{5,3},{7,1},{8,14},{10,12},{12... | collective-permute-start | bytes 1572872 | tf_op jit(solution)/shard_map/ppermute | solution.py:183
  131.6 24.1 %copy-start = (bf16[4,16,128,128]{3,2,1,0:T(8,128)(2,1)}, bf16[4,16,128,128]{3,2,1,0:T(8,128)(2,1)S(1)}, u32[]{:S(2)}) copy-start(bf16[4,16,128,128]{3,2,1,0:T(8,128)(2,1)S(1)} %all-to-all-done.2) | copy-start | bytes 6291460
  131.6 35.3 %all-to-all-start.4 = ((bf16[16,136,128]{2,1,0:T(8,128)(2,1)}), bf16[16,136,128]{2,1,0:T(8,128)(2,1)S(1)}, u32[]{:S(2)}, u32[]{:S(2)}) async-start(bf16[16,136,128]{2,1,0:T(8,128)(2,1)} %bitcast.41), calls=%async_computation.4 | async-start | bytes 1114112 | tf_op jit(solution)/shard_map/all_to_all | solution.py:25
  136.2 16.5 %collective-permute-start.12 = (bf16[2,2,32,2048]{3,2,1,0:T(8,128)(2,1)S(1)}, bf16[2,2,32,2048]{3,2,1,0:T(8,128)(2,1)S(1)}, u32[]{:S(2)}, u32[]{:S(2)}) collective-permute-start(bf16[2,2,32,2048]{3,2,1,0:T(8,128)(2,1)S(1)} %bitcast.45), channel_id=1, source_target_pairs={{0,1},{1,0},{2,3},{3,2},{4,5},{5,4},{6,7},{7,6},{8,9},{9,8},{10,11... | collective-permute-start | bytes 1572872 | tf_op jit(solution)/shard_map/ppermute | solution.py:21
  150.8 4.0 %collective-permute-start.13 = (bf16[2,2,32,2048]{3,2,1,0:T(8,128)(2,1)}, bf16[2,2,32,2048]{3,2,1,0:T(8,128)(2,1)S(1)}, u32[]{:S(2)}, u32[]{:S(2)}) collective-permute-start(bf16[2,2,32,2048]{3,2,1,0:T(8,128)(2,1)} %collective-permute-done.11.refs_10_), channel_id=1, source_target_pairs={{0,1},{1,0},{2,3},{3,2},{4,5},{5,4},{6,7},{7,6},{8,9},{9,8},{10,11... | collective-permute-start | bytes 1572872 | tf_op jit(solution)/shard_map/ppermute | solution.py:21
  164.6 31.2 %copy-start.15 = (f32[8]{0:T(128)S(1)}, f32[8]{0:T(128)}, u32[]{:S(2)}) copy-start(f32[8]{0:T(128)} %param.11) | copy-start | bytes 100
  164.7 7.3 %collective-permute-start.14 = (bf16[8,32,256]{2,1,0:T(8,128)(2,1)}, bf16[8,32,256]{2,1,0:T(8,128)(2,1)S(1)}, u32[]{:S(2)}, u32[]{:S(2)}) collective-permute-start(bf16[8,32,256]{2,1,0:T(8,128)(2,1)} %get-tuple-element.5), channel_id=1, source_target_pairs={{0,1},{1,0},{2,3},{3,2},{4,5},{5,4},{6,7},{7,6},{8,9},{9,8},{10,11... | collective-permute-start | bytes 393224 | tf_op jit(solution)/shard_map/ppermute | solution.py:21
  167.6 12.2 %all-to-all-start.5 = ((f32[4,8,128]{2,1,0:T(8,128)}), f32[4,8,128]{2,1,0:T(8,128)S(1)}, u32[]{:S(2)}, u32[]{:S(2)}) async-start(f32[4,8,128]{2,1,0:T(8,128)} %broadcast_in_dim.34), calls=%async_computation.5 | async-start | bytes 32768 | tf_op jit(solution)/shard_map/all_to_all | solution.py:25
  (14 other events, 145.4 us)

commit v3 on v2

--- a/solution.py
+++ b/solution.py
@@ -129,7 +129,7 @@
             total += crossed[s * part : (s + 1) * part, s * block : (s + 1) * block]
         first, second = total[:width], total[width:]
         keep[k] = jnp.where(c == 0, first, second)
-        give[k] = jnp.where(c == 0, second, first).astype(jnp.bfloat16)
+        give[k] = jnp.where(c == 0, second, first)
 
 
 def whole(intersect_left, stored_block, stored_site, current_site, current_block, penalty_weight):
@@ -205,7 +205,7 @@
         grow_kernel,
         out_shape=(
             jax.ShapeDtypeStruct((states, width, block), jnp.float32),
-            jax.ShapeDtypeStruct((states, width, block), jnp.bfloat16),
+            jax.ShapeDtypeStruct((states, width, block), jnp.float32),
         ),
         in_specs=[resident] * 9 + [anywhere] * 4 + [resident],
         out_specs=(resident, resident),
@@ -218,7 +218,7 @@
         name="grow",
     )(*pieces, site_pair, site_far, site_pair_other, site_far_other, spread)
     got = shifted(give, CORE, 1)
-    grown = (keep + got.astype(jnp.float32)).astype(jnp.bfloat16)
+    grown = (keep + got).astype(jnp.bfloat16)
 
     total = jnp.broadcast_to(total[:, :1], (states, block))
     high = lax.reduce_precision(total, 8, 7)

time: 199 us -> 199 us (level)
  no operation moved by 1% of the time
where the time goes in v3:
time: 199 us; the launch traced here: 198 us
  starting transfers between devices  84.9 us (43%)
  waiting for transfers between devices  66.8 us (34%)
  Pallas kernels  15.8 us (8%)
  blocking collectives  15.8 us (8%)
  local copies, waits for them, and re-layouts  12 us (6%)
    ppermute x14, starting transfers between devices, shifted(): lax.ppermute(value, axis, [(i, (i + step) % size) for i in range(size)])  40.6 us
    all_to_all x6, starting transfers between devices, exchanged(): return lax.all_to_all(value, axis, split_axis=0, concat_axis=0, tiled=True)  38.4 us
    all_to_all x6, waiting for transfers between devices, exchanged(): return lax.all_to_all(value, axis, split_axis=0, concat_axis=0, tiled=True)  21.4 us
    ppermute x14, waiting for transfers between devices, shifted(): lax.ppermute(value, axis, [(i, (i + step) % size) for i in range(size)])  17 us
    ppermute x1, waiting for transfers between devices, whole(): other = lax.ppermute(mine, column, [(i, 3 - i) for i in range(4)])  15.9 us
    all_to_all x1, blocking collectives, exchanged(): return lax.all_to_all(value, axis, split_axis=0, concat_axis=0, tiled=True)  15.8 us
    ppermute x1, waiting for transfers between devices, whole(): lax.ppermute(site_pair, (FAR, NEAR), [(i, 3 - i) for i in range(4)])  12.5 us
    pallas_call x1, Pallas kernels, whole(): pl.pallas_call(grow_kernel, out_shape=(jax.ShapeDtypeStruct((states, widt...  9.05 us
  transfers between devices with their start and end apart: 22, of which 9 were waited for; matrix products, arithmetic and copies ran while one was open for 3% of the time, Pallas kernels for 8%

profile of v3, /device:TPU:10, one launch (start us, length us, event | category | flops | bytes accessed | tf_op | source)
XLA Modules:
  0.0 197.7 jit_solution(11706177609053588371)
XLA Ops:
  2.3 6.2 %all-to-all-start = ((bf16[4,32,128]{2,1,0:T(8,128)(2,1)}), bf16[4,32,128]{2,1,0:T(8,128)(2,1)S(1)}, u32[]{:S(2)}, u32[]{:S(2)}) async-start(bf16[4,32,128]{2,1,0:T(8,128)(2,1)} %reshape.117), calls=%async_computation | async-start | bytes 65536 | tf_op jit(solution)/shard_map/all_to_all | solution.py:25
  9.5 6.9 %all-to-all-done = bf16[4,32,128]{2,1,0:T(8,128)(2,1)S(1)} async-done(((bf16[4,32,128]{2,1,0:T(8,128)(2,1)}), bf16[4,32,128]{2,1,0:T(8,128)(2,1)S(1)}, u32[]{:S(2)}, u32[]{:S(2)}) %all-to-all-start) | async-done | bytes 32800 | tf_op jit(solution)/shard_map/all_to_all | solution.py:25
  17.3 6.2 %all-to-all-start.3 = ((bf16[16,128,128]{2,1,0:T(8,128)(2,1)}), bf16[16,128,128]{2,1,0:T(8,128)(2,1)S(1)}, u32[]{:S(2)}, u32[]{:S(2)}) async-start(bf16[16,128,128]{2,1,0:T(8,128)(2,1)} %bitcast.17), calls=%async_computation.3 | async-start | bytes 1048576 | tf_op jit(solution)/shard_map/all_to_all | solution.py:25
  23.5 2.5 %collective-permute-start = (bf16[32,2048]{1,0:T(8,128)(2,1)S(1)}, bf16[32,2048]{1,0:T(8,128)(2,1)S(1)}, u32[]{:S(2)}, u32[]{:S(2)}) collective-permute-start(bf16[32,2048]{1,0:T(8,128)(2,1)S(1)} %bitcast.48), channel_id=1, source_target_pairs={{0,2},{2,0},{1,3},{3,1},{4,6},{6,4},{5,7},{7,5},{8,10},{10,8},{9,1... | collective-permute-start | bytes 393224 | tf_op jit(solution)/shard_map/ppermute | solution.py:21
  26.0 6.8 %all-to-all-done.3 = bf16[16,128,128]{2,1,0:T(8,128)(2,1)S(1)} async-done(((bf16[16,128,128]{2,1,0:T(8,128)(2,1)}), bf16[16,128,128]{2,1,0:T(8,128)(2,1)S(1)}, u32[]{:S(2)}, u32[]{:S(2)}) %all-to-all-start.3) | async-done | bytes 524320 | tf_op jit(solution)/shard_map/all_to_all | solution.py:25
  33.7 11.3 %all-to-all-start.1 = ((bf16[16,128,128]{2,1,0:T(8,128)(2,1)}), bf16[16,128,128]{2,1,0:T(8,128)(2,1)S(1)}, u32[]{:S(2)}, u32[]{:S(2)}) async-start(bf16[16,128,128]{2,1,0:T(8,128)(2,1)} %broadcast_in_dim.31), calls=%async_computation.1 | async-start | bytes 1048576 | tf_op jit(solution)/shard_map/all_to_all | solution.py:25
  47.1 15.9 %collective-permute-done.1 = bf16[2,32,2048]{2,1,0:T(8,128)(2,1)S(1)} collective-permute-done((bf16[2,32,2048]{2,1,0:T(8,128)(2,1)S(1)}, bf16[2,32,2048]{2,1,0:T(8,128)(2,1)S(1)}, u32[]{:S(2)}, u32[]{:S(2)}) %collective-permute-start.1) | collective-permute-done | bytes 262176 | tf_op jit(solution)/shard_map/ppermute | solution.py:154
  63.1 3.6 %collective-permute-start.2 = (bf16[128,2048]{1,0:T(8,128)(2,1)S(1)}, bf16[128,2048]{1,0:T(8,128)(2,1)S(1)}, u32[]{:S(2)}, u32[]{:S(2)}) collective-permute-start(bf16[128,2048]{1,0:T(8,128)(2,1)S(1)} %bitcast.37), channel_id=1, source_target_pairs={{0,8},{8,16},{16,24},{24,32},{32,40},{40,48},{48,56},{56,0},{1,9},... | collective-permute-start | bytes 1572872 | tf_op jit(solution)/shard_map/ppermute | solution.py:21
  66.6 3.5 %collective-permute-start.3 = (bf16[128,2048]{1,0:T(8,128)(2,1)S(1)}, bf16[128,2048]{1,0:T(8,128)(2,1)}, u32[]{:S(2)}, u32[]{:S(2)}) collective-permute-start(bf16[128,2048]{1,0:T(8,128)(2,1)S(1)} %bitcast.38), channel_id=1, source_target_pairs={{0,56},{8,0},{16,8},{24,16},{32,24},{40,32},{48,40},{56,48},{1,57}... | collective-permute-start | bytes 1572872 | tf_op jit(solution)/shard_map/ppermute | solution.py:21
  72.0 5.6 %all-to-all-start.2 = ((bf16[4,16,128,128]{3,2,1,0:T(8,128)(2,1)}), bf16[4,16,128,128]{3,2,1,0:T(8,128)(2,1)S(1)}, u32[]{:S(2)}, u32[]{:S(2)}) async-start(bf16[4,16,128,128]{3,2,1,0:T(8,128)(2,1)} %broadcast_in_dim.32), calls=%async_computation.2 | async-start | bytes 4194304 | tf_op jit(solution)/shard_map/all_to_all | solution.py:25
  77.6 2.4 %collective-permute-done.2.refs_1_ = bf16[128,2048]{1,0:T(8,128)(2,1)S(1)} collective-permute-done((bf16[128,2048]{1,0:T(8,128)(2,1)S(1)}, bf16[128,2048]{1,0:T(8,128)(2,1)S(1)}, u32[]{:S(2)}, u32[]{:S(2)}) %collective-permute-start.2) | collective-permute-done | bytes 524320 | tf_op jit(solution)/shard_map/ppermute | solution.py:21
  82.4 4.7 %collective-permute-start.5 = (bf16[128,2048]{1,0:T(8,128)(2,1)}, bf16[128,2048]{1,0:T(8,128)(2,1)S(1)}, u32[]{:S(2)}, u32[]{:S(2)}) collective-permute-start(bf16[128,2048]{1,0:T(8,128)(2,1)} %collective-permute-done.3.refs_2_), channel_id=1, source_target_pairs={{0,56},{8,0},{16,8},{24,16},{32,24},{40,32},{48,40},{56,48},{1,57}... | collective-permute-start | bytes 1572872 | tf_op jit(solution)/shard_map/ppermute | solution.py:21
  87.1 9.0 %collective-permute-done.4.refs_3_ = bf16[128,2048]{1,0:T(8,128)(2,1)S(1)} collective-permute-done((bf16[128,2048]{1,0:T(8,128)(2,1)S(1)}, bf16[128,2048]{1,0:T(8,128)(2,1)S(1)}, u32[]{:S(2)}, u32[]{:S(2)}) %collective-permute-start.4) | collective-permute-done | bytes 524320 | tf_op jit(solution)/shard_map/ppermute | solution.py:21
  98.1 5.1 %collective-permute-start.7 = (bf16[128,2048]{1,0:T(8,128)(2,1)S(1)}, bf16[128,2048]{1,0:T(8,128)(2,1)S(1)}, u32[]{:S(2)}, u32[]{:S(2)}) collective-permute-start(bf16[128,2048]{1,0:T(8,128)(2,1)S(1)} %collective-permute-done.5.refs_4_), channel_id=1, source_target_pairs={{0,56},{8,0},{16,8},{24,16},{32,24},{40,32},{48,40},{56,48},{1,57}... | collective-permute-start | bytes 1572872 | tf_op jit(solution)/shard_map/ppermute | solution.py:21
  107.1 4.3 %collective-permute-done.6.refs_5_ = bf16[128,2048]{1,0:T(8,128)(2,1)S(1)} collective-permute-done((bf16[128,2048]{1,0:T(8,128)(2,1)S(1)}, bf16[128,2048]{1,0:T(8,128)(2,1)S(1)}, u32[]{:S(2)}, u32[]{:S(2)}) %collective-permute-start.6) | collective-permute-done | bytes 524320 | tf_op jit(solution)/shard_map/ppermute | solution.py:21
  114.9 5.1 %collective-permute-start.9 = (bf16[64,2048]{1,0:T(8,128)(2,1)}, bf16[64,2048]{1,0:T(8,128)(2,1)}, u32[]{:S(2)}, u32[]{:S(2)}) collective-permute-start(bf16[64,2048]{1,0:T(8,128)(2,1)} %slice.29), channel_id=1, source_target_pairs={{0,56},{8,0},{16,8},{24,16},{32,24},{40,32},{48,40},{56,48},{1,57}... | collective-permute-start | bytes 786440 | tf_op jit(solution)/shard_map/ppermute | solution.py:21
  121.9 4.0 %collective-permute-start.11 = (bf16[2,2,32,2048]{3,2,1,0:T(8,128)(2,1)}, bf16[2,2,32,2048]{3,2,1,0:T(8,128)(2,1)}, u32[]{:S(2)}, u32[]{:S(2)}) collective-permute-start(bf16[2,2,32,2048]{3,2,1,0:T(8,128)(2,1)} %bitcast.43), channel_id=1, source_target_pairs={{0,6},{2,4},{4,2},{6,0},{1,7},{3,5},{5,3},{7,1},{8,14},{10,12},{12... | collective-permute-start | bytes 1572872 | tf_op jit(solution)/shard_map/ppermute | solution.py:183
  126.7 4.9 %project.1 = bf16[8,2,136,128]{3,2,1,0:T(8,128)(2,1)} custom-call(bf16[128,2048]{1,0:T(8,128)(2,1)} %bitcast.39, bf16[128,2048]{1,0:T(8,128)(2,1)} %copy-done.4, bf16[128,2048]{1,0:T(8,128)(2,1)} %collective-permute-done.3.refs_2_, bf16[128,2048]{1,0:T(8,128)(2,1)} %copy-done.5, bf16[128,2048]{1,0:T(8,128)(2,1)} %copy-done.6, bf16[128,2048]{1,0:T(8,128)(2,1)} %copy-done.2, ...), custom_call_target="tpu_custom_call" | custom-call | flops 1073741824 | bytes 5242880 | tf_op jit(solution)/shard_map/project/pallas_call | solution.py:190
  131.6 4.7 %all-to-all-start.4 = ((bf16[16,136,128]{2,1,0:T(8,128)(2,1)}), bf16[16,136,128]{2,1,0:T(8,128)(2,1)S(1)}, u32[]{:S(2)}, u32[]{:S(2)}) async-start(bf16[16,136,128]{2,1,0:T(8,128)(2,1)} %bitcast.41), calls=%async_computation.4 | async-start | bytes 1114112 | tf_op jit(solution)/shard_map/all_to_all | solution.py:25
  138.3 12.5 %collective-permute-done.11.refs_10_ = bf16[2,2,32,2048]{3,2,1,0:T(8,128)(2,1)} collective-permute-done((bf16[2,2,32,2048]{3,2,1,0:T(8,128)(2,1)}, bf16[2,2,32,2048]{3,2,1,0:T(8,128)(2,1)}, u32[]{:S(2)}, u32[]{:S(2)}) %collective-permute-start.11) | collective-permute-done | bytes 524320 | tf_op jit(solution)/shard_map/ppermute | solution.py:183
  155.6 9.1 %grow.1 = (f32[8,32,256]{2,1,0:T(8,128)}, f32[8,32,256]{2,1,0:T(8,128)}) custom-call(bf16[128,2048]{1,0:T(8,128)(2,1)} %bitcast.40, bf16[128,2048]{1,0:T(8,128)(2,1)} %copy-done.4, bf16[128,2048]{1,0:T(8,128)(2,1)} %collective-permute-done.3.refs_2_, bf16[128,2048]{1,0:T(8,128)(2,1)} %copy-done.5, bf16[128,2048]{1,0:T(8,128)(2,1)} %copy-done.6, ...), custom_call_target="tpu_custom_call" | custom-call | flops 1610612736 | bytes 6291456 | tf_op jit(solution)/shard_map/grow/pallas_call | solution.py:204
  167.6 4.4 %all-to-all-start.5 = ((f32[4,8,128]{2,1,0:T(8,128)}), f32[4,8,128]{2,1,0:T(8,128)S(1)}, u32[]{:S(2)}, u32[]{:S(2)}) async-start(f32[4,8,128]{2,1,0:T(8,128)} %broadcast_in_dim.34), calls=%async_computation.5 | async-start | bytes 32768 | tf_op jit(solution)/shard_map/all_to_all | solution.py:25
  172.0 7.7 %all-to-all-done.5 = f32[4,8,128]{2,1,0:T(8,128)S(1)} async-done(((f32[4,8,128]{2,1,0:T(8,128)}), f32[4,8,128]{2,1,0:T(8,128)S(1)}, u32[]{:S(2)}, u32[]{:S(2)}) %all-to-all-start.5) | async-done | bytes 16416 | tf_op jit(solution)/shard_map/all_to_all | solution.py:25
  180.0 15.8 %all_to_all.35 = bf16[8,40,256]{2,1,0:T(8,128)(2,1)S(1)} all-to-all(bf16[8,40,256]{2,1,0:T(8,128)(2,1)S(1)} %pad_maximum_fusion), channel_id=1, replica_groups=mesh['state_0'=2,'state_1'=4,'bond_0'=8,'bond_1'=2,'bond_2'=2,'bond_3'=2..., dimensions={0} | all-to-all | bytes 327680 | tf_op jit(solution)/shard_map/all_to_all | solution.py:25
  (90 shorter events, 34.4 us)
Async XLA Ops:
  2.3 14.1 %all-to-all-start = ((bf16[4,32,128]{2,1,0:T(8,128)(2,1)}), bf16[4,32,128]{2,1,0:T(8,128)(2,1)S(1)}, u32[]{:S(2)}, u32[]{:S(2)}) async-start(bf16[4,32,128]{2,1,0:T(8,128)(2,1)} %reshape.117), calls=%async_computation | async-start | bytes 65536 | tf_op jit(solution)/shard_map/all_to_all | solution.py:25
  17.3 15.5 %all-to-all-start.3 = ((bf16[16,128,128]{2,1,0:T(8,128)(2,1)}), bf16[16,128,128]{2,1,0:T(8,128)(2,1)S(1)}, u32[]{:S(2)}, u32[]{:S(2)}) async-start(bf16[16,128,128]{2,1,0:T(8,128)(2,1)} %bitcast.17), calls=%async_computation.3 | async-start | bytes 1048576 | tf_op jit(solution)/shard_map/all_to_all | solution.py:25
  23.5 21.5 %collective-permute-start = (bf16[32,2048]{1,0:T(8,128)(2,1)S(1)}, bf16[32,2048]{1,0:T(8,128)(2,1)S(1)}, u32[]{:S(2)}, u32[]{:S(2)}) collective-permute-start(bf16[32,2048]{1,0:T(8,128)(2,1)S(1)} %bitcast.48), channel_id=1, source_target_pairs={{0,2},{2,0},{1,3},{3,1},{4,6},{6,4},{5,7},{7,5},{8,10},{10,8},{9,1... | collective-permute-start | bytes 393224 | tf_op jit(solution)/shard_map/ppermute | solution.py:21
  33.7 36.4 %all-to-all-start.1 = ((bf16[16,128,128]{2,1,0:T(8,128)(2,1)}), bf16[16,128,128]{2,1,0:T(8,128)(2,1)S(1)}, u32[]{:S(2)}, u32[]{:S(2)}) async-start(bf16[16,128,128]{2,1,0:T(8,128)(2,1)} %broadcast_in_dim.31), calls=%async_computation.1 | async-start | bytes 1048576 | tf_op jit(solution)/shard_map/all_to_all | solution.py:25
  45.1 17.9 %collective-permute-start.1 = (bf16[2,32,2048]{2,1,0:T(8,128)(2,1)S(1)}, bf16[2,32,2048]{2,1,0:T(8,128)(2,1)S(1)}, u32[]{:S(2)}, u32[]{:S(2)}) collective-permute-start(bf16[2,32,2048]{2,1,0:T(8,128)(2,1)S(1)} %maximum_select_fusion.2), channel_id=1, source_target_pairs={{0,6},{2,4},{4,2},{6,0},{1,7},{3,5},{5,3},{7,1},{8,14},{10,12},{12... | collective-permute-start | bytes 786440 | tf_op jit(solution)/shard_map/ppermute | solution.py:154
  63.1 17.0 %collective-permute-start.2 = (bf16[128,2048]{1,0:T(8,128)(2,1)S(1)}, bf16[128,2048]{1,0:T(8,128)(2,1)S(1)}, u32[]{:S(2)}, u32[]{:S(2)}) collective-permute-start(bf16[128,2048]{1,0:T(8,128)(2,1)S(1)} %bitcast.37), channel_id=1, source_target_pairs={{0,8},{8,16},{16,24},{24,32},{32,40},{40,48},{48,56},{56,0},{1,9},... | collective-permute-start | bytes 1572872 | tf_op jit(solution)/shard_map/ppermute | solution.py:21
  66.6 15.7 %collective-permute-start.3 = (bf16[128,2048]{1,0:T(8,128)(2,1)S(1)}, bf16[128,2048]{1,0:T(8,128)(2,1)}, u32[]{:S(2)}, u32[]{:S(2)}) collective-permute-start(bf16[128,2048]{1,0:T(8,128)(2,1)S(1)} %bitcast.38), channel_id=1, source_target_pairs={{0,56},{8,0},{16,8},{24,16},{32,24},{40,32},{48,40},{56,48},{1,57}... | collective-permute-start | bytes 1572872 | tf_op jit(solution)/shard_map/ppermute | solution.py:21
  72.0 59.5 %all-to-all-start.2 = ((bf16[4,16,128,128]{3,2,1,0:T(8,128)(2,1)}), bf16[4,16,128,128]{3,2,1,0:T(8,128)(2,1)S(1)}, u32[]{:S(2)}, u32[]{:S(2)}) async-start(bf16[4,16,128,128]{3,2,1,0:T(8,128)(2,1)} %broadcast_in_dim.32), calls=%async_computation.2 | async-start | bytes 4194304 | tf_op jit(solution)/shard_map/all_to_all | solution.py:25
  80.0 16.1 %collective-permute-start.4 = (bf16[128,2048]{1,0:T(8,128)(2,1)S(1)}, bf16[128,2048]{1,0:T(8,128)(2,1)S(1)}, u32[]{:S(2)}, u32[]{:S(2)}) collective-permute-start(bf16[128,2048]{1,0:T(8,128)(2,1)S(1)} %collective-permute-done.2.refs_1_), channel_id=1, source_target_pairs={{0,8},{8,16},{16,24},{24,32},{32,40},{40,48},{48,56},{56,0},{1,9},... | collective-permute-start | bytes 1572872 | tf_op jit(solution)/shard_map/ppermute | solution.py:21
  82.4 15.7 %collective-permute-start.5 = (bf16[128,2048]{1,0:T(8,128)(2,1)}, bf16[128,2048]{1,0:T(8,128)(2,1)S(1)}, u32[]{:S(2)}, u32[]{:S(2)}) collective-permute-start(bf16[128,2048]{1,0:T(8,128)(2,1)} %collective-permute-done.3.refs_2_), channel_id=1, source_target_pairs={{0,56},{8,0},{16,8},{24,16},{32,24},{40,32},{48,40},{56,48},{1,57}... | collective-permute-start | bytes 1572872 | tf_op jit(solution)/shard_map/ppermute | solution.py:21
  96.2 15.3 %collective-permute-start.6 = (bf16[128,2048]{1,0:T(8,128)(2,1)S(1)}, bf16[128,2048]{1,0:T(8,128)(2,1)S(1)}, u32[]{:S(2)}, u32[]{:S(2)}) collective-permute-start(bf16[128,2048]{1,0:T(8,128)(2,1)S(1)} %collective-permute-done.4.refs_3_), channel_id=1, source_target_pairs={{0,8},{8,16},{16,24},{24,32},{32,40},{40,48},{48,56},{56,0},{1,9},... | collective-permute-start | bytes 1572872 | tf_op jit(solution)/shard_map/ppermute | solution.py:21
  98.1 16.0 %collective-permute-start.7 = (bf16[128,2048]{1,0:T(8,128)(2,1)S(1)}, bf16[128,2048]{1,0:T(8,128)(2,1)S(1)}, u32[]{:S(2)}, u32[]{:S(2)}) collective-permute-start(bf16[128,2048]{1,0:T(8,128)(2,1)S(1)} %collective-permute-done.5.refs_4_), channel_id=1, source_target_pairs={{0,56},{8,0},{16,8},{24,16},{32,24},{40,32},{48,40},{56,48},{1,57}... | collective-permute-start | bytes 1572872 | tf_op jit(solution)/shard_map/ppermute | solution.py:21
  103.2 22.7 %collective-permute-start.15 = (bf16[128,2048]{1,0:T(8,128)(2,1)}, bf16[128,2048]{1,0:T(8,128)(2,1)}, u32[]{:S(2)}, u32[]{:S(2)}) collective-permute-start(bf16[128,2048]{1,0:T(8,128)(2,1)} %bitcast.46), channel_id=1, source_target_pairs={{0,1},{1,0},{2,3},{3,2},{4,5},{5,4},{6,7},{7,6},{8,9},{9,8},{10,11... | collective-permute-start | bytes 1572872 | tf_op jit(solution)/shard_map/ppermute | solution.py:21
  105.2 14.9 %collective-permute-start.10 = (bf16[64,2048]{1,0:T(8,128)(2,1)}, bf16[64,2048]{1,0:T(8,128)(2,1)}, u32[]{:S(2)}, u32[]{:S(2)}) collective-permute-start(bf16[64,2048]{1,0:T(8,128)(2,1)} %bitcast.6.refs_0_), channel_id=1, source_target_pairs={{0,2},{2,0},{1,3},{3,1},{4,6},{6,4},{5,7},{7,5},{8,10},{10,8},{9,1... | collective-permute-start | bytes 786440 | tf_op jit(solution)/shard_map/ppermute | solution.py:21
  112.2 13.7 %collective-permute-start.8 = (bf16[64,2048]{1,0:T(8,128)(2,1)}, bf16[64,2048]{1,0:T(8,128)(2,1)S(1)}, u32[]{:S(2)}, u32[]{:S(2)}) collective-permute-start(bf16[64,2048]{1,0:T(8,128)(2,1)} %slice.28), channel_id=1, source_target_pairs={{0,8},{8,16},{16,24},{24,32},{32,40},{40,48},{48,56},{56,0},{1,9},... | collective-permute-start | bytes 786440 | tf_op jit(solution)/shard_map/ppermute | solution.py:21
  114.9 11.0 %collective-permute-start.9 = (bf16[64,2048]{1,0:T(8,128)(2,1)}, bf16[64,2048]{1,0:T(8,128)(2,1)}, u32[]{:S(2)}, u32[]{:S(2)}) collective-permute-start(bf16[64,2048]{1,0:T(8,128)(2,1)} %slice.29), channel_id=1, source_target_pairs={{0,56},{8,0},{16,8},{24,16},{32,24},{40,32},{48,40},{56,48},{1,57}... | collective-permute-start | bytes 786440 | tf_op jit(solution)/shard_map/ppermute | solution.py:21
  121.9 28.8 %collective-permute-start.11 = (bf16[2,2,32,2048]{3,2,1,0:T(8,128)(2,1)}, bf16[2,2,32,2048]{3,2,1,0:T(8,128)(2,1)}, u32[]{:S(2)}, u32[]{:S(2)}) collective-permute-start(bf16[2,2,32,2048]{3,2,1,0:T(8,128)(2,1)} %bitcast.43), channel_id=1, source_target_pairs={{0,6},{2,4},{4,2},{6,0},{1,7},{3,5},{5,3},{7,1},{8,14},{10,12},{12... | collective-permute-start | bytes 1572872 | tf_op jit(solution)/shard_map/ppermute | solution.py:183
  131.6 24.1 %copy-start = (bf16[4,16,128,128]{3,2,1,0:T(8,128)(2,1)}, bf16[4,16,128,128]{3,2,1,0:T(8,128)(2,1)S(1)}, u32[]{:S(2)}) copy-start(bf16[4,16,128,128]{3,2,1,0:T(8,128)(2,1)S(1)} %all-to-all-done.2) | copy-start | bytes 6291460
  131.6 35.3 %all-to-all-start.4 = ((bf16[16,136,128]{2,1,0:T(8,128)(2,1)}), bf16[16,136,128]{2,1,0:T(8,128)(2,1)S(1)}, u32[]{:S(2)}, u32[]{:S(2)}) async-start(bf16[16,136,128]{2,1,0:T(8,128)(2,1)} %bitcast.41), calls=%async_computation.4 | async-start | bytes 1114112 | tf_op jit(solution)/shard_map/all_to_all | solution.py:25
  136.2 16.5 %collective-permute-start.12 = (bf16[2,2,32,2048]{3,2,1,0:T(8,128)(2,1)S(1)}, bf16[2,2,32,2048]{3,2,1,0:T(8,128)(2,1)S(1)}, u32[]{:S(2)}, u32[]{:S(2)}) collective-permute-start(bf16[2,2,32,2048]{3,2,1,0:T(8,128)(2,1)S(1)} %bitcast.45), channel_id=1, source_target_pairs={{0,1},{1,0},{2,3},{3,2},{4,5},{5,4},{6,7},{7,6},{8,9},{9,8},{10,11... | collective-permute-start | bytes 1572872 | tf_op jit(solution)/shard_map/ppermute | solution.py:21
  150.8 4.0 %collective-permute-start.13 = (bf16[2,2,32,2048]{3,2,1,0:T(8,128)(2,1)}, bf16[2,2,32,2048]{3,2,1,0:T(8,128)(2,1)S(1)}, u32[]{:S(2)}, u32[]{:S(2)}) collective-permute-start(bf16[2,2,32,2048]{3,2,1,0:T(8,128)(2,1)} %collective-permute-done.11.refs_10_), channel_id=1, source_target_pairs={{0,1},{1,0},{2,3},{3,2},{4,5},{5,4},{6,7},{7,6},{8,9},{9,8},{10,11... | collective-permute-start | bytes 1572872 | tf_op jit(solution)/shard_map/ppermute | solution.py:21
  164.7 7.3 %collective-permute-start.14 = (f32[8,32,256]{2,1,0:T(8,128)}, f32[8,32,256]{2,1,0:T(8,128)S(1)}, u32[]{:S(2)}, u32[]{:S(2)}) collective-permute-start(f32[8,32,256]{2,1,0:T(8,128)} %get-tuple-element.5), channel_id=1, source_target_pairs={{0,1},{1,0},{2,3},{3,2},{4,5},{5,4},{6,7},{7,6},{8,9},{9,8},{10,11... | collective-permute-start | bytes 786440 | tf_op jit(solution)/shard_map/ppermute | solution.py:21
  167.0 29.0 %copy-start.15 = (f32[8]{0:T(128)S(1)}, f32[8]{0:T(128)}, u32[]{:S(2)}) copy-start(f32[8]{0:T(128)} %param.11) | copy-start | bytes 100
  167.6 12.2 %all-to-all-start.5 = ((f32[4,8,128]{2,1,0:T(8,128)}), f32[4,8,128]{2,1,0:T(8,128)S(1)}, u32[]{:S(2)}, u32[]{:S(2)}) async-start(f32[4,8,128]{2,1,0:T(8,128)} %broadcast_in_dim.34), calls=%async_computation.5 | async-start | bytes 32768 | tf_op jit(solution)/shard_map/all_to_all | solution.py:25
  (14 other events, 145.4 us)
